TPU v7x, 16 devices: a 4x2x1 block of a 4x4x8 slice. The times are simulated.
16 devices in a mesh: dp: 2 (over y, z), fsdp: 8 (over x, core).
Axes of the slice: x: 4, y: 2, z: 1, core: 2. Of those that a mesh axis runs over, the one named last changes fastest.
The devices are a block of a 4x4x8 slice.
Arguments:
- hidden: bfloat16 [48, 768, 2048], P(('dp', 'fsdp')), parts along dimension 0
- g_attn: bfloat16 [2048], P('fsdp')
- w_query: bfloat16 [2048, 2048], P('fsdp')
- w_key: bfloat16 [2048, 256], P('fsdp')
- w_value: bfloat16 [2048, 256], P('fsdp')
- w_out: bfloat16 [2048, 2048], P('fsdp')
- g_mlp: bfloat16 [2048], P('fsdp')
- w_gate: bfloat16 [2048, 11008], P('fsdp')
- w_up: bfloat16 [2048, 11008], P('fsdp')
- w_down: bfloat16 [11008, 2048], P('fsdp')
- cos_tab: float32 [768, 64], replicated
- sin_tab: float32 [768, 64], replicated
Outputs:
- output 1: bfloat16 [48, 768, 2048], P(('dp', 'fsdp')), parts along dimension 0
- output 2: bfloat16 [48, 768, 2, 128], P(('dp', 'fsdp')), parts along dimension 0
- output 3: bfloat16 [48, 768, 2, 128], P(('dp', 'fsdp')), parts along dimension 0
There are 2 independent parts. A program takes and returns all parts, laid end to end along the dimension named above; an argument that names none is the same for every part.
All inputs are finite; a program needn't handle non-finite values.
Results may differ from a plain program's by a relative error of at most 0.0191086.
Values are sent between devices in bfloat16 or wider.
A program may use at most 768 MiB of HBM per device.

v0:
```python
import functools
import jax
import jax.numpy as jnp
from jax import lax
from jax.sharding import PartitionSpec as P

NORM_EPS = 1e-5
QUERY_BLOCK = 256


def rms_norm(rows_in, gain_vec):
    upcast = rows_in.astype(jnp.float32)
    scaled = upcast * lax.rsqrt(jnp.mean(upcast * upcast, axis=-1, keepdims=True) + NORM_EPS)
    return (scaled * gain_vec.astype(jnp.float32)).astype(jnp.bfloat16)


def apply_rope(heads_in, cos_tab, sin_tab):
    half_dim = cos_tab.shape[-1]
    upcast = heads_in.astype(jnp.float32)
    lo_half = upcast[..., :half_dim]
    hi_half = upcast[..., half_dim:]
    cos_bc = cos_tab[:, None, :]
    sin_bc = sin_tab[:, None, :]
    rotated = jnp.concatenate([lo_half * cos_bc - hi_half * sin_bc, hi_half * cos_bc + lo_half * sin_bc], axis=-1)
    return rotated.astype(jnp.bfloat16)


def causal_attention(query_grp, key_rot, value_heads):
    seq_len = query_grp.shape[1]
    head_dim = query_grp.shape[-1]
    blk_len = min(QUERY_BLOCK, seq_len)
    out_blocks = []
    for blk_start in range(0, seq_len, blk_len):
        blk_stop = blk_start + blk_len
        scores = jnp.einsum("bqkgd,bskd->bkgqs", query_grp[:, blk_start:blk_stop], key_rot[:, :blk_stop], preferred_element_type=jnp.float32) * head_dim ** -0.5
        allowed = (blk_start + jnp.arange(blk_len))[:, None] >= jnp.arange(blk_stop)[None, :]
        scores = jnp.where(allowed, scores, -jnp.inf)
        prob_bf16 = jax.nn.softmax(scores, axis=-1).astype(jnp.bfloat16)
        out_blocks.append(jnp.einsum("bkgqs,bskd->bqkgd", prob_bf16, value_heads[:, :blk_stop], preferred_element_type=jnp.float32).astype(jnp.bfloat16))
    return jnp.concatenate(out_blocks, axis=1)


def decoder_layer(hidden, g_attn, w_query, w_key, w_value, w_out, g_mlp, w_gate, w_up, w_down, cos_tab, sin_tab):
    num_seqs = hidden.shape[0]
    seq_len = hidden.shape[1]
    head_dim = 2 * cos_tab.shape[1]
    num_heads = w_query.shape[1] // head_dim
    kv_heads = w_key.shape[1] // head_dim
    normed = rms_norm(hidden, g_attn)
    query_proj = jnp.dot(normed, w_query, preferred_element_type=jnp.float32).astype(jnp.bfloat16)
    key_proj = jnp.dot(normed, w_key, preferred_element_type=jnp.float32).astype(jnp.bfloat16)
    value_proj = jnp.dot(normed, w_value, preferred_element_type=jnp.float32).astype(jnp.bfloat16)
    query_rot = apply_rope(query_proj.reshape(num_seqs, seq_len, num_heads, head_dim), cos_tab, sin_tab)
    key_rot = apply_rope(key_proj.reshape(num_seqs, seq_len, kv_heads, head_dim), cos_tab, sin_tab)
    value_heads = value_proj.reshape(num_seqs, seq_len, kv_heads, head_dim)
    query_grp = query_rot.reshape(num_seqs, seq_len, kv_heads, num_heads // kv_heads, head_dim)
    attn_heads = causal_attention(query_grp, key_rot, value_heads)
    attn_flat = attn_heads.reshape(num_seqs, seq_len, num_heads * head_dim)
    attn_proj = jnp.dot(attn_flat, w_out, preferred_element_type=jnp.float32).astype(jnp.bfloat16)
    residual = (hidden.astype(jnp.float32) + attn_proj.astype(jnp.float32)).astype(jnp.bfloat16)
    normed_mlp = rms_norm(residual, g_mlp)
    gate_proj = jnp.dot(normed_mlp, w_gate, preferred_element_type=jnp.float32).astype(jnp.bfloat16)
    up_proj = jnp.dot(normed_mlp, w_up, preferred_element_type=jnp.float32).astype(jnp.bfloat16)
    act_in = (jax.nn.silu(gate_proj.astype(jnp.float32)) * up_proj.astype(jnp.float32)).astype(jnp.bfloat16)
    mlp_out = jnp.dot(act_in, w_down, preferred_element_type=jnp.float32).astype(jnp.bfloat16)
    out_hidden = (residual.astype(jnp.float32) + mlp_out.astype(jnp.float32)).astype(jnp.bfloat16)
    return out_hidden, key_rot, value_heads


def solution(mesh):
    tok_spec = P(("dp", "fsdp"), None, None)
    cache_spec = P(("dp", "fsdp"), None, None, None)
    row_spec = P("fsdp", None)
    gain_spec = P("fsdp")
    table_spec = P(None, None)
    gather_rows = functools.partial(lax.all_gather, axis_name="fsdp", axis=0, tiled=True)

    def local_layer(hidden, g_attn, w_query, w_key, w_value, w_out, g_mlp, w_gate, w_up, w_down, cos_tab, sin_tab):
        return decoder_layer(hidden, gather_rows(g_attn), gather_rows(w_query), gather_rows(w_key), gather_rows(w_value), gather_rows(w_out), gather_rows(g_mlp), gather_rows(w_gate), gather_rows(w_up), gather_rows(w_down), cos_tab, sin_tab)

    return jax.shard_map(local_layer, mesh=mesh, in_specs=(tok_spec, gain_spec, row_spec, row_spec, row_spec, row_spec, gain_spec, row_spec, row_spec, row_spec, table_spec, table_spec), out_specs=(tok_spec, cache_spec, cache_spec), check_vma=False)
```

profile of v0, /device:TPU:112, one launch (start us, length us, event | category | flops | bytes accessed | tf_op | source)
XLA Modules:
  0.0 887.1 jit_solution(3193501914072067807)
XLA Ops:
  14.4 24.3 %all-gather = bf16[8,1,256]{2,1,0:T(2,128)(2,1)S(1)} all-gather(bf16[1,1,256]{2,1,0:T(2,128)(2,1)S(1)} %reshape.61), channel_id=1, replica_groups=mesh['dp'=2,'fsdp'=8] {'fsdp'}, dimensions={0}, use_global_device_ids=true | all-gather | bytes 4608 | tf_op jit(solution)/shard_map/all_gather | solution.py:79
  39.1 21.1 %all-gather.1 = bf16[8,1,256]{2,1,0:T(2,128)(2,1)S(1)} all-gather(bf16[1,1,256]{2,1,0:T(2,128)(2,1)S(1)} %reshape.63), channel_id=1, replica_groups=mesh['dp'=2,'fsdp'=8] {'fsdp'}, dimensions={0}, use_global_device_ids=true | all-gather | bytes 4608 | tf_op jit(solution)/shard_map/all_gather | solution.py:79
  61.4 5.6 fusion.21
  68.6 6.7 fusion.77
  75.5 2.1 copy.57
  77.5 1.9 copy.58
  79.4 3.0 subtract_convert_fusion.1
  83.1 2.2 copy.45
  85.3 7.8 fusion.74
  93.1 4.8 copy.46
  97.9 4.3 all-gather.14.cloned.1.call-done
  102.2 26.7 %convert_convert_fusion = f32[3,768,2048]{2,1,0:T(8,128)} fusion(bf16[2048,2048]{1,0:T(8,128)(2,1)} %all-gather.14.cloned.1.call-done, bf16[3,768,2048]{2,1,0:T(8,128)(2,1)} %param.12, f32[2048]{0:T(1024)} %bitcast.151, f32[3,768]{1,0:T(4,128)S(1)} %add_rsqrt_fusion.1), kind=kOutput, calls=%fused_computation.53 | convolution fusion | flops 19355664384 | bytes 36717568 | tf_op jit(solution)/shard_map/dot_general | solution.py:50
  128.9 10.4 %copy.59 = f32[288,8,16,128]{3,2,1,0:T(8,128)S(1)} copy(f32[288,8,16,128]{3,1,2,0:T(8,128)} %bitcast.140) | data formatting | bytes 37748736
  139.3 9.7 %subtract_convert_fusion = (bf16[3,768,16,64]{3,2,1,0:T(8,128)(2,1)}, bf16[3,768,16,64]{3,2,1,0:T(8,128)(2,1)}) fusion(f32[3,768,16,128]{3,2,1,0:T(8,128)S(1)} %bitcast.133, f32[768,64]{1,0:T(8,128)S(1)} %copy-done.4, f32[768,64]{1,0:T(8,128)S(1)} %copy-done.2), kind=kLoop, calls=%fused_computation.41 | loop fusion | flops 18874368 | bytes 28704768 | tf_op jit(solution)/shard_map/convert.5
  149.0 9.8 %copy.39 = bf16[3,768,16,64]{3,1,2,0:T(8,128)(2,1)} copy(bf16[3,768,16,64]{3,2,1,0:T(8,128)(2,1)} %get-tuple-element.9) | data formatting | bytes 9437184 | tf_op jit(solution)/shard_map/convert.5
  158.8 9.8 %copy.40 = bf16[3,768,16,64]{3,1,2,0:T(8,128)(2,1)} copy(bf16[3,768,16,64]{3,2,1,0:T(8,128)(2,1)} %get-tuple-element.10) | data formatting | bytes 9437184 | tf_op jit(solution)/shard_map/convert.4
  168.7 9.7 %fusion.72 = f32[3,2,256,256,8]{3,2,4,1,0:T(8,128)} fusion(bf16[3,768,2,8,64]{4,1,3,2,0:T(8,128)(2,1)} %bitcast.134, bf16[3,768,2,8,64]{4,1,3,2,0:T(8,128)(2,1)} %bitcast.137, bf16[3,768,2,64]{3,1,2,0:T(8,128)(2,1)S(1)} %get-tuple-element.11, bf16[3,768,2,64]{3,1,2,0:T(8,128)(2,1)S(1)} %get-tuple-element.12), kind=kOutput, calls=%fused_computation.72 | convolution fusion | flops 812384256 | bytes 23199744 | tf_op jit(solution)/shard_map/bqkgd,bskd->bkgqs/dot_general | solution.py:35
  178.4 13.8 %fusion.69 = f32[3,2,512,256,8]{3,2,4,1,0:T(8,128)} fusion(bf16[3,768,2,8,64]{4,1,3,2,0:T(8,128)(2,1)S(1)} %bitcast.136, bf16[3,768,2,8,64]{4,1,3,2,0:T(8,128)(2,1)} %bitcast.138, bf16[3,768,2,64]{3,1,2,0:T(8,128)(2,1)S(1)} %get-tuple-element.11, bf16[3,768,2,64]{3,1,2,0:T(8,128)(2,1)S(1)} %get-tuple-element.12), kind=kOutput, calls=%fused_computation.70 | convolution fusion | flops 1618477056 | bytes 35782656 | tf_op jit(solution)/shard_map/bqkgd,bskd->bkgqs/dot_general | solution.py:35
  192.2 11.0 %fusion.111 = (f32[3,2,8,256]{3,2,1,0:T(8,128)S(1)}, f32[3,2,8,256,256]{3,4,2,1,0:T(8,128)S(1)}) fusion(f32[3,2,256,256,8]{3,2,4,1,0:T(8,128)} %fusion.72, pred[256,256]{0,1:T(8,128)(4,1)S(1)} %copy-done.11), kind=kOutput, calls=%fused_computation.116 | output fusion | flops 18874624 | bytes 25280512 | tf_op jit(solution)/shard_map/sub | solution.py:38
  203.2 2.9 convert_bitcast_fusion.2
  206.2 20.2 %fusion.105 = (f32[3,2,8,256]{3,2,1,0:T(8,128)}, f32[3,2,8,256,768]{3,4,2,1,0:T(8,128)}) fusion(pred[256,768]{0,1:T(8,128)(4,1)S(1)} %copy-done.7, bf16[3,768,2,128]{3,1,2,0:T(8,128)(2,1)S(1)} %pad_maximum_fusion.2, bf16[3,768,2,8,64]{4,1,3,2,0:T(8,128)(2,1)} %bitcast.139, bf16[3,768,2,8,64]{4,1,3,2,0:T(8,128)(2,1)} %bitcast.135), kind=kOutput, calls=%fused_computation.114 | convolution fusion | flops 2459960064 | bytes 48611328 | tf_op jit(solution)/shard_map/sub | solution.py:38
  226.4 32.3 %fusion.110 = (f32[3,2,8,256]{3,2,1,0:T(8,128)S(1)}, f32[3,2,8,256,512]{3,4,2,1,0:T(8,128)}) fusion(f32[3,2,512,256,8]{3,2,4,1,0:T(8,128)} %fusion.69, pred[256,512]{0,1:T(8,128)(4,1)S(1)} %copy-done.10), kind=kOutput, calls=%fused_computation.115 | output fusion | flops 37749248 | bytes 50511872 | tf_op jit(solution)/shard_map/sub | solution.py:38
  258.7 11.7 %convert_bitcast_fusion.1 = bf16[3,256,2,8,128]{1,4,3,2,0:T(8,128)(2,1)} fusion(f32[3,2,8,256,512]{3,4,2,1,0:T(8,128)} %get-tuple-element.18, f32[3,2,8,256]{3,2,1,0:T(8,128)S(1)} %get-tuple-element.17, bf16[3,768,2,128]{1,3,2,0:T(8,128)(2,1)S(1)} %bitcast.146), kind=kOutput, calls=%fused_computation.75 | convolution fusion | flops 1624768512 | bytes 29147136 | tf_op jit(solution)/shard_map/bkgqs,bskd->bqkgd/dot_general | solution.py:39
  270.5 15.5 %convert_bitcast_fusion = bf16[3,256,2,8,128]{1,4,3,2,0:T(8,128)(2,1)} fusion(bf16[3,768,2,128,1]{1,3,4,2,0:T(8,128)(2,1)} %bitcast.144, f32[3,2,8,256,768]{3,4,2,1,0:T(8,128)} %get-tuple-element.16, f32[3,2,8,256]{3,2,1,0:T(8,128)S(1)} %copy-done.16), kind=kOutput, calls=%fused_computation.74 | convolution fusion | flops 2436366336 | bytes 42123264 | tf_op jit(solution)/shard_map/bkgqs,bskd->bqkgd/dot_general | solution.py:39
  286.0 6.7 pad_maximum_fusion
  292.7 28.8 %fusion.25 = (f32[3,768]{1,0:T(4,128)S(1)}, bf16[3,768,2048]{2,1,0:T(8,128)(2,1)}) fusion(bf16[3,768,2048]{1,2,0:T(8,128)(2,1)} %bitcast.141, bf16[2048,2048]{1,0:T(8,128)(2,1)} %all-gather.16.cloned.1.call-done, bf16[3,768,2048]{2,1,0:T(8,128)(2,1)} %param.12), kind=kOutput, calls=%fused_computation.34 | convolution fusion | flops 19365099520 | bytes 36709376 | tf_op jit(solution)/shard_map/dot_general | solution.py:59
  321.6 31.7 %all-gather.20.cloned.1.call-done = bf16[2048,11008]{1,0:T(8,128)(2,1)} async-done(((bf16[256,11008]{1,0:T(8,128)(2,1)}), bf16[2048,11008]{1,0:T(8,128)(2,1)}) %all-gather.20.cloned.1.call-update) | async-done | bytes 45088784 | tf_op jit(solution)/shard_map/all_gather | solution.py:79
  353.3 119.7 %fusion.11 = bf16[3,768,11008]{2,1,0:T(8,128)(2,1)} fusion(bf16[2048,11008]{1,0:T(8,128)(2,1)} %all-gather.20.cloned.1.call-done, bf16[3,768,2048]{2,1,0:T(8,128)(2,1)} %get-tuple-element.22, f32[2048]{0:T(1024)S(1)} %bitcast.147, f32[3,768]{1,0:T(4,128)S(1)} %add_rsqrt_fusion), kind=kOutput, calls=%fused_computation.12 | convolution fusion | flops 103903395840 | bytes 105268224 | tf_op jit(solution)/shard_map/dot_general | solution.py:63
  473.0 83.4 %all-gather.18.cloned.1.call-done = bf16[2048,11008]{1,0:T(8,128)(2,1)} async-done(((bf16[256,11008]{1,0:T(8,128)(2,1)}), bf16[2048,11008]{1,0:T(8,128)(2,1)}) %all-gather.18.cloned.1.call-update) | async-done | bytes 45088784 | tf_op jit(solution)/shard_map/all_gather | solution.py:79
  556.4 137.3 %fusion.126 = bf16[3,768,11008]{2,1,0:T(8,128)(2,1)} fusion(bf16[3,768,11008]{2,1,0:T(8,128)(2,1)} %fusion.11, bf16[2048,11008]{1,0:T(8,128)(2,1)} %all-gather.18.cloned.1.call-done, bf16[3,768,2048]{2,1,0:T(8,128)(2,1)} %get-tuple-element.22, f32[2048]{0:T(1024)S(1)} %bitcast.148, f32[3,768]{1,0:T(4,128)S(1)} %add_rsqrt_fusion), kind=kOutput, calls=%fused_computation.9.clone.clone.clone.clone.1 | convolution fusion | flops 104131657728 | bytes 155993088 | tf_op jit(solution)/shard_map/dot_general | solution.py:62
  693.7 66.0 %all-gather.22.cloned.1.call-done = bf16[11008,2048]{1,0:T(8,128)(2,1)} async-done(((bf16[1376,2048]{1,0:T(8,128)(2,1)}), bf16[11008,2048]{1,0:T(8,128)(2,1)}) %all-gather.22.cloned.1.call-update) | async-done | bytes 45088784 | tf_op jit(solution)/shard_map/all_gather | solution.py:79
  759.7 120.3 %fusion.28 = bf16[3,768,2048]{2,1,0:T(8,128)(2,1)} fusion(bf16[3,768,2048]{2,1,0:T(8,128)(2,1)} %get-tuple-element.22, bf16[11008,2048]{1,0:T(8,128)(2,1)} %all-gather.22.cloned.1.call-done, bf16[3,768,11008]{2,1,0:T(8,128)(2,1)} %fusion.126), kind=kOutput, calls=%fused_computation.37 | convolution fusion | flops 103908114432 | bytes 114688000 | tf_op jit(solution)/shard_map/dot_general | solution.py:65
  (68 shorter events, 11.1 us)
Async XLA Ops:
  7.2 61.4 %all-gather.12.cloned.1.call-start = ((), (), s32[]{:S(2)}) async-start(), calls=%async_computation.1 | async-start | bytes 1179648 | tf_op jit(solution)/shard_map/all_gather | solution.py:79
  9.0 76.3 %all-gather.10.cloned.1.call-start = ((), (), s32[]{:S(2)}) async-start(), calls=%async_computation | async-start | bytes 1179648 | tf_op jit(solution)/shard_map/all_gather | solution.py:79
  10.8 3.6 copy-start.14
  10.8 27.9 %copy-start.8 = (f32[768,64]{0,1:T(8,128)S(1)}, f32[768,64]{0,1:T(8,128)}, u32[]{:S(2)}) copy-start(f32[768,64]{0,1:T(8,128)} %param.22) | copy-start | bytes 589828
  10.8 91.4 %all-gather.14.cloned.1.call-start = ((), (), s32[]{:S(2)}) async-start(), calls=%async_computation.2 | async-start | bytes 9437184 | tf_op jit(solution)/shard_map/all_gather | solution.py:79
  11.6 27.2 %copy-start.9 = (f32[768,64]{0,1:T(8,128)S(1)}, f32[768,64]{0,1:T(8,128)}, u32[]{:S(2)}) copy-start(f32[768,64]{0,1:T(8,128)} %param.23) | copy-start | bytes 589828
  11.6 27.4 %copy-start.15 = (bf16[256]{0:T(256)(128)(2,1)S(1)}, bf16[256]{0:T(256)(128)(2,1)}, u32[]{:S(2)}) copy-start(bf16[256]{0:T(256)(128)(2,1)} %param.18) | copy-start | bytes 1540
  11.6 281.1 %all-gather.16.cloned.1.call-start = ((), (), s32[]{:S(2)}) async-start(), calls=%async_computation.3 | async-start | bytes 9437184 | tf_op jit(solution)/shard_map/all_gather | solution.py:79
  12.3 341.0 %all-gather.20.cloned.1.call-start = ((), (), s32[]{:S(2)}) async-start(), calls=%async_computation.5 | async-start | bytes 50724864 | tf_op jit(solution)/shard_map/all_gather | solution.py:79
  12.9 543.5 %all-gather.18.cloned.1.call-start = ((), (), s32[]{:S(2)}) async-start(), calls=%async_computation.4 | async-start | bytes 50724864 | tf_op jit(solution)/shard_map/all_gather | solution.py:79
  13.5 746.2 %all-gather.22.cloned.1.call-start = ((), (), s32[]{:S(2)}) async-start(), calls=%async_computation.6 | async-start | bytes 50724864 | tf_op jit(solution)/shard_map/all_gather | solution.py:79
  38.7 36.6 %copy-start.13 = (f32[8,1,256]{2,1,0:T(1,128)}, f32[8,1,256]{2,1,0:T(1,128)S(1)}, u32[]{:S(2)}) copy-start(f32[8,1,256]{2,1,0:T(1,128)S(1)} %convert_element_type.139) | copy-start | bytes 24580
  38.8 40.6 %copy-start.1 = (f32[768,64]{1,0:T(8,128)}, f32[768,64]{1,0:T(8,128)S(1)}, u32[]{:S(2)}) copy-start(f32[768,64]{1,0:T(8,128)S(1)} %copy.34) | copy-start | bytes 589828
  39.0 40.4 %copy-start.3 = (f32[768,64]{1,0:T(8,128)}, f32[768,64]{1,0:T(8,128)S(1)}, u32[]{:S(2)}) copy-start(f32[768,64]{1,0:T(8,128)S(1)} %copy.36) | copy-start | bytes 589828
  128.9 10.4 %copy-start.2 = (f32[768,64]{1,0:T(8,128)S(1)}, f32[768,64]{1,0:T(8,128)}, u32[]{:S(2)}) copy-start(f32[768,64]{1,0:T(8,128)} %copy-done.1) | copy-start | bytes 589828
  128.9 10.4 %copy-start.4 = (f32[768,64]{1,0:T(8,128)S(1)}, f32[768,64]{1,0:T(8,128)}, u32[]{:S(2)}) copy-start(f32[768,64]{1,0:T(8,128)} %copy-done.3) | copy-start | bytes 589828
  168.7 9.7 %copy-start = (bf16[3,768,16,64]{3,1,2,0:T(8,128)(2,1)S(1)}, bf16[3,768,16,64]{3,1,2,0:T(8,128)(2,1)}, u32[]{:S(2)}) copy-start(bf16[3,768,16,64]{3,1,2,0:T(8,128)(2,1)} %copy.39) | copy-start | bytes 14155780
  178.4 13.8 %copy-start.11 = (pred[256,256]{0,1:T(8,128)(4,1)S(1)}, pred[256,256]{0,1:T(8,128)(4,1)}, u32[]{:S(2)}) copy-start(pred[256,256]{0,1:T(8,128)(4,1)} %iota_compare_fusion.2) | copy-start | bytes 196612
  192.2 11.1 %copy-start.6 = (bf16[3,768,256]{1,2,0:T(8,128)(2,1)S(1)}, bf16[3,768,256]{1,2,0:T(8,128)(2,1)}, u32[]{:S(2)}) copy-start(bf16[3,768,256]{1,2,0:T(8,128)(2,1)} %fusion.74) | copy-start | bytes 3538948
  203.2 2.9 copy-start.7
  206.1 20.2 %copy-start.10 = (pred[256,512]{0,1:T(8,128)(4,1)S(1)}, pred[256,512]{0,1:T(8,128)(4,1)}, u32[]{:S(2)}) copy-start(pred[256,512]{0,1:T(8,128)(4,1)} %iota_compare_fusion.1) | copy-start | bytes 393220
  258.7 11.7 %copy-start.16 = (f32[3,2,8,256]{3,2,1,0:T(8,128)S(1)}, f32[3,2,8,256]{3,2,1,0:T(8,128)}, u32[]{:S(2)}) copy-start(f32[3,2,8,256]{3,2,1,0:T(8,128)} %get-tuple-element.15) | copy-start | bytes 147460
  270.5 15.5 %copy-start.5 = (bf16[3,256,2,8,128]{1,4,3,2,0:T(8,128)(2,1)S(1)}, bf16[3,256,2,8,128]{1,4,3,2,0:T(8,128)(2,1)}, u32[]{:S(2)}) copy-start(bf16[3,256,2,8,128]{1,4,3,2,0:T(8,128)(2,1)} %convert_bitcast_fusion.2) | copy-start | bytes 9437188
  292.7 60.6 %copy-start.12 = (f32[8,1,256]{2,1,0:T(1,128)S(1)}, f32[8,1,256]{2,1,0:T(1,128)}, u32[]{:S(2)}) copy-start(f32[8,1,256]{2,1,0:T(1,128)} %convert_element_type.140) | copy-start | bytes 24580
Sparse Core Ops, SparseCore 0:
  10.1 21.8 all-gather.11
  34.2 19.9 all-gather.9
  55.9 46.2 all-gather.13
  103.7 45.6 all-gather.15
  150.8 202.4 all-gather.19
  354.7 201.6 all-gather.17
  558.0 201.6 all-gather.21
where the time goes:
time: 894 us; the launch traced here: 887 us
  matrix products  521 us (58%)
  waiting for transfers between devices  189 us (21%)
  other arithmetic  71.9 us (8%)
  blocking collectives  45.4 us (5%)
  local copies, waits for them, and re-layouts  45 us (5%)
  between operations  14.6 us (2%)
    dot_general x1, matrix products, decoder_layer(): jnp.dot(normed_mlp, w_gate, preferred_element_type=jnp.float32)  137 us
    dot_general x1, matrix products, decoder_layer(): jnp.dot(act_in, w_down, preferred_element_type=jnp.float32)  120 us
    dot_general x1, matrix products, decoder_layer(): jnp.dot(normed_mlp, w_up, preferred_element_type=jnp.float32)  120 us
    all_gather x1, waiting for transfers between devices, local_layer(): gather_rows(w_gate)  83.4 us
    all_gather x1, waiting for transfers between devices, local_layer(): gather_rows(w_down)  66 us
    sub x2, other arithmetic, causal_attention(): prob_bf16 = jax.nn.softmax(scores, axis=-1).astype(jnp.bfloat16)  43.4 us
    all_gather x1, waiting for transfers between devices, local_layer(): gather_rows(w_up)  31.7 us
    dot_general x3, matrix products, causal_attention(): jnp.einsum('bkgqs,bskd->bqkgd', prob_bf16, value_heads[:, :blk_stop], pre...  30.1 us
  transfers between devices with their start and end apart: 7, of which 4 were waited for; matrix products, arithmetic and copies ran while one was open for 58% of the time, Pallas kernels for 0%

commit v1 on v0

v1 whole, which is shorter than its diff:
```python
import functools, math
import jax, jax.numpy as jnp
from jax import lax
from jax.experimental import pallas as pl
from jax.experimental.pallas import tpu as pltpu
from jax.sharding import PartitionSpec as P

F32 = jnp.float32
BF = jnp.bfloat16
MESH = pl.DeviceIdType.MESH
HBM = pltpu.MemorySpace.HBM
EPS = 1e-5


class Group:
    def __init__(self, name, local, col0, outer, common, rows, nblk):
        self.name, self.local, self.col0 = name, local, col0
        self.outer, self.common, self.rows, self.nblk = outer, common, rows, nblk
        self.width = 2 * outer + common

    def shape(self):
        return jax.ShapeDtypeStruct((self.rows * self.nblk, self.width), BF)


def place(nblk):
    me = lax.axis_index("fsdp")
    dp = lax.axis_index("dp")
    core = lax.rem(me, 2)
    chip = me // 2
    chips = nblk // 2
    par = lax.rem(dp, 2)
    blk = lambda k: lax.rem(chip + k, chips) * 2 + core
    return dict(me=me, par=par, core=core,
                left=blk(chips - 1), right=blk(1), far=blk(2), mate=me + 1 - 2 * core,
                dev_left=(dp, blk(chips - 1)), dev_right=(dp, blk(1)), dev_mate=(dp, me + 1 - 2 * core),
                dev_pair=(dp + 1 - 2 * par, me))


def stage_copies(g, stage, at, loc, full):
    R, H, m, mc = g.rows, g.rows // 2, g.outer, g.outer + g.common
    par = at["par"]
    cols = lambda start, n: pl.ds(pl.multiple_of(start, 128), n)
    rows = lambda b, o=0, n=R: pl.ds(pl.multiple_of(b * R + o, 16), n)
    xr, mine, theirs = cols(par * m, mc), cols(par * mc, m), cols((1 - par) * mc, m)
    if stage == 1:
        src = loc.at[:, cols(g.col0 + par * m, mc)]
        own = rows(at["me"])
        return [(src, full.at[own, xr], at["dev_right"]), (src, full.at[own, xr], at["dev_left"]),
                (loc.at[:, pl.ds(g.col0, g.width)], full.at[own, :], at["dev_mate"])]
    same = lambda r, c, dev: (full.at[r, c], full.at[r, c], dev)
    lo, hi, far, mate = at["left"], at["right"], at["far"], at["mate"]
    allc = pl.ds(0, g.width)
    if stage == 2:
        out = [same(rows(lo, 0, H), xr, at["dev_right"]), same(rows(hi, H, H), xr, at["dev_left"])]
        if m:
            out += [same(rows(lo), mine, at["dev_pair"]), same(rows(hi), mine, at["dev_pair"])]
        return out + [same(rows(lo), xr, at["dev_mate"]), same(rows(hi), xr, at["dev_mate"]), same(rows(mate), allc, at["dev_mate"])]
    if stage == 3:
        out = []
        if m:
            out += [same(rows(far), mine, at["dev_pair"])]
        out += [same(rows(far), xr, at["dev_mate"])]
        if m:
            out += [same(rows(lo), theirs, at["dev_mate"]), same(rows(hi), theirs, at["dev_mate"])]
        return out
    return [same(rows(far), theirs, at["dev_mate"])] if m else []


def n_copies(g, stage):
    m = g.outer > 0
    return {1: 3, 2: 7 if m else 5, 3: 4 if m else 1, 4: 1 if m else 0}[stage]


def call(name, cid, body, grid, ins, in_specs, outs, out_specs, ticks, bufs, locs, nblk, flops=0, nbytes=0, scratch=(), alias=None):
    groups = []
    for _, acts in ticks:
        for g, s in acts:
            if g not in groups:
                groups.append(g)
    old = [g for g in groups if g.name in bufs]
    new = [g for g in groups if g.name not in bufs]
    lnames = []
    for _, acts in ticks:
        for g, s in acts:
            if s == 1 and g.local not in lnames:
                lnames.append(g.local)
    base, total = {}, 0
    for _, acts in ticks:
        for g, s in acts:
            base[(g.name, s)] = total
            total += n_copies(g, s)
    nsteps = math.prod(grid)
    n_in, n_out, n_sc = len(ins), len(outs), len(scratch)

    def kernel(*refs):
        cin, refs = refs[:n_in], refs[n_in:]
        lrefs, refs = refs[:len(lnames)], refs[len(lnames):]
        refs = refs[len(old):]
        couts, refs = refs[:n_out], refs[n_out:]
        gref, refs = refs[:len(groups)], refs[len(groups):]
        sc, refs = refs[:n_sc], refs[n_sc:]
        if not total:
            body(cin, couts, sc)
            return
        ssem, rsem = refs
        full = {g.name: r for g, r in zip(old + new, gref)}
        loc = dict(zip(lnames, lrefs))
        step = pl.program_id(0)
        for k in range(1, len(grid)):
            step = step * grid[k] + pl.program_id(k)
        at = place(nblk)

        def copies(g, s):
            b = base[(g.name, s)]
            return [pltpu.make_async_remote_copy(src_ref=a, dst_ref=d, send_sem=ssem.at[b + k], recv_sem=rsem.at[b + k],
                                                 device_id=dev, device_id_type=MESH)
                    for k, (a, d, dev) in enumerate(stage_copies(g, s, at, loc.get(g.local), full[g.name]))]

        got = set()
        for n, (when, acts) in enumerate(ticks):
            need = []
            for g, s in acts:
                if (g.name, s - 1) in base and (g.name, s - 1) not in got:
                    need.append((g, s - 1))
                    got.add((g.name, s - 1))

            @pl.when(step == when)
            def _():
                if n == 0:
                    bar = pltpu.get_barrier_semaphore()
                    for dev in ("dev_left", "dev_right", "dev_mate", "dev_pair"):
                        pl.semaphore_signal(bar, inc=1, device_id=at[dev], device_id_type=MESH)
                    pl.semaphore_wait(bar, 4)
                for g, s in need:
                    for cp in copies(g, s):
                        cp.wait_recv()
                for g, s in acts:
                    for cp in copies(g, s):
                        cp.start()

        body(cin, couts, sc)

        @pl.when(step == nsteps - 1)
        def _():
            for _, acts in ticks:
                for g, s in acts:
                    for cp in copies(g, s):
                        if (g.name, s) not in got:
                            cp.wait_recv()
                        cp.wait_send()

    hb = pl.BlockSpec(memory_space=HBM)
    al = dict(alias or {})
    for k in range(len(old)):
        al[n_in + len(lnames) + k] = n_out + k
    res = pl.pallas_call(
        kernel, grid=grid,
        in_specs=list(in_specs) + [hb] * (len(lnames) + len(old)),
        out_specs=list(out_specs) + [hb] * len(groups),
        out_shape=list(outs) + [g.shape() for g in old + new],
        scratch_shapes=list(scratch) + ([pltpu.SemaphoreType.DMA((total,)), pltpu.SemaphoreType.DMA((total,))] if total else []),
        input_output_aliases=al,
        compiler_params=pltpu.CompilerParams(vmem_limit_bytes=62 << 20, **(dict(collective_id=cid, has_side_effects=True) if total else {})),
        cost_estimate=pl.CostEstimate(flops=flops, bytes_accessed=nbytes, transcendentals=0),
        name=name)(*ins, *[locs[n] for n in lnames], *[bufs[g.name] for g in old])
    for g, b in zip(old + new, res[n_out:]):
        bufs[g.name] = b
    return res[:n_out]


def norm_body(cin, couts, sc):
    x_ref, g_ref = cin
    x = x_ref[...].astype(F32)
    r = lax.rsqrt(jnp.mean(x * x, axis=-1, keepdims=True) + EPS)
    couts[0][...] = (x * r * g_ref[...].astype(F32)).astype(BF)


def qkv_body(qw, kw, cin, couts, sc):
    h_ref, *w_refs, cos_ref, sin_ref = cin
    q_ref, k_ref, v_ref = couts
    hd = cos_ref.shape[1]
    c, s = cos_ref[...], sin_ref[...]
    col = 0
    for w_ref in w_refs:
        for n0 in range(0, w_ref.shape[1], 2 * hd):
            acc = jnp.dot(h_ref[...], w_ref[:, n0:n0 + 2 * hd], preferred_element_type=F32).astype(BF)
            for j in (0, hd):
                part = acc[:, j:j + hd]
                if col < qw + kw:
                    t = part.astype(F32)
                    part = (t * c + pltpu.roll(t, hd // 2, 1) * s).astype(BF)
                if col < qw:
                    q_ref[:, col:col + hd] = part
                elif col < qw + kw:
                    k_ref[:, col - qw:col - qw + hd] = part
                else:
                    v_ref[:, col - qw - kw:col - qw - kw + hd] = part
                col += hd


def attn_body(hd, qb, unroll, cin, couts, sc):
    q_ref, k_ref, v_ref = cin
    o_ref, = couts
    S, nh = q_ref.shape[0], q_ref.shape[1] // hd
    scale = hd ** -0.5 * math.log2(math.e)
    mask = lax.broadcasted_iota(jnp.int32, (qb, qb), 0) >= lax.broadcasted_iota(jnp.int32, (qb, qb), 1)

    def one(head):
        hs = pl.ds(pl.multiple_of(head * hd, hd), hd)
        for b in range(S // qb):
            n = (b + 1) * qb
            qq = q_ref[b * qb:n, hs]
            s = lax.dot_general(qq, k_ref[:n, :], (((1,), (1,)), ((), ())), preferred_element_type=F32)
            diag = jnp.where(mask, s[:, b * qb:], -jnp.inf)
            s = diag if b == 0 else jnp.concatenate([s[:, :b * qb], diag], axis=1)
            p = jnp.exp2((s - jnp.max(s, axis=1, keepdims=True)) * scale)
            pb = (p * (1.0 / jnp.sum(p, axis=1, keepdims=True))).astype(BF)
            o_ref[b * qb:n, hs] = jnp.dot(pb, v_ref[:n, :], preferred_element_type=F32).astype(BF)

    def step(i, _):
        for u in range(unroll):
            one(i * unroll + u)
        return 0
    lax.fori_loop(0, nh // unroll, step, 0)


def wout_body(cin, couts, sc):
    *o_refs, w_ref, x_ref, g_ref = cin
    x1_ref, h_ref = couts
    D = w_ref.shape[1]
    o = jnp.concatenate([r[...] for r in o_refs], axis=1)
    ss = jnp.zeros((o.shape[0], 1), F32)
    step = min(512, D)
    for n0 in range(0, D, step):
        cs = slice(n0, n0 + step)
        a = jnp.dot(o, w_ref[:, cs], preferred_element_type=F32).astype(BF)
        x1 = (x_ref[:, cs].astype(F32) + a.astype(F32)).astype(BF)
        x1_ref[:, cs] = x1
        xf = x1.astype(F32)
        ss = ss + jnp.sum(xf * xf, axis=1, keepdims=True)
    r = lax.rsqrt(ss / D + EPS)
    for n0 in range(0, D, step):
        cs = slice(n0, n0 + step)
        h_ref[:, cs] = (x1_ref[:, cs].astype(F32) * r * g_ref[:, cs].astype(F32)).astype(BF)


def gu_body(mt, cin, couts, sc):
    h_ref, wg_ref, wu_ref = cin[:3]
    r_ref, = couts

    def step(i, _):
        rs = pl.ds(pl.multiple_of(i * mt, mt), mt)
        hh = h_ref[rs, :]
        g = jnp.dot(hh, wg_ref[...], preferred_element_type=F32).astype(BF).astype(F32)
        u = jnp.dot(hh, wu_ref[...], preferred_element_type=F32).astype(BF).astype(F32)
        r_ref[rs, :] = ((g / (1.0 + jnp.exp(-g))) * u).astype(BF)
        return 0
    lax.fori_loop(0, h_ref.shape[0] // mt, step, 0)


def down_body(cin, couts, sc):
    r_ref, w_ref, x_ref = cin[:3]
    m = jnp.dot(r_ref[...], w_ref[...], preferred_element_type=F32).astype(BF)
    couts[0][...] = (x_ref[...].astype(F32) + m.astype(F32)).astype(BF)


UNIT = 256
GU_UNITS = (6, 6, 6, 6, 6, 6, 7)
DOWN_COLS = (512, 512, 512, 512)


def thirds(cols, unit, frac=1 / 3):
    outer = int(cols // unit * frac + 0.5) * unit
    return outer, cols - 2 * outer


def local_layer(nblk, hidden, g_attn, w_query, w_key, w_value, w_out, g_mlp, w_gate, w_up, w_down, cos_tab, sin_tab):
    B, S, D = hidden.shape
    T = B * S
    hd = 2 * cos_tab.shape[1]
    qw, kw = w_query.shape[1], w_key.shape[1]
    ff = w_gate.shape[1]
    kv = kw // hd
    x = hidden.reshape(T, D)
    gains = lax.all_gather(jnp.stack([g_attn, g_mlp]), "fsdp", axis=1, tiled=True)
    ga, gm = gains[0:1], gains[1:2]
    cos2 = jnp.concatenate([cos_tab, cos_tab], axis=1)
    sin2 = jnp.concatenate([-sin_tab, sin_tab], axis=1)
    locs = dict(wq=jnp.concatenate([w_query, w_key, w_value], axis=1), wo=w_out, wg=w_gate, wu=w_up, wd=w_down)
    rw = w_query.shape[0]
    qk = qw + 2 * kw
    half = qk // 2
    Q = [Group("q%d" % k, "wq", k * half, *thirds(half, 128, .2), rw, nblk) for k in range(2)]
    WO = Group("wo", "wo", 0, *thirds(D, 128), rw, nblk)
    G, c0 = [], 0
    for k, u in enumerate(GU_UNITS):
        G.append([Group("g%d" % k, "wg", c0, *thirds(u * UNIT, 128), rw, nblk), Group("u%d" % k, "wu", c0, *thirds(u * UNIT, 128), rw, nblk)])
        c0 += u * UNIT
    assert c0 == ff
    Dn, c0 = [], 0
    for k, w in enumerate(DOWN_COLS):
        Dn.append(Group("d%d" % k, "wd", c0, *thirds(w, 128), w_down.shape[0], nblk))
        c0 += w
    assert c0 == D
    seq = [[g] if isinstance(g, Group) else g for g in G + Dn]

    def acts(i):
        out = []
        for s in (2, 3, 4, 1):
            if 0 <= i - (s - 1) < len(seq):
                out += [(g, s) for g in seq[i - (s - 1)] if n_copies(g, s)]
        return out

    bufs = {}
    run = functools.partial(call, bufs=bufs, locs=locs, nblk=nblk)
    sd = jax.ShapeDtypeStruct
    mt = 256
    row = lambda i: (i, 0)
    const = lambda *a: (0, 0)
    cid = 0
    h, = run("gather_norm", cid, norm_body, (T // mt,), [x, ga], [pl.BlockSpec((mt, D), row), pl.BlockSpec((1, D), const)],
             [sd((T, D), BF)], [pl.BlockSpec((mt, D), row)],
             [(0, [(Q[0], 1), (Q[1], 1)]), (1, [(Q[0], 2)]), (2, [(Q[1], 2)]), (3, [(WO, 1)]), (4, [(Q[0], 3)]), (5, [(Q[1], 3)]), (6, [(Q[0], 4), (Q[1], 4)])])
    tab = pl.BlockSpec((mt, hd), lambda i: (i % (S // mt), 0))
    cid += 1
    q, k, v = run("qkv", cid, functools.partial(qkv_body, qw, kw), (T // mt,), [h, bufs["q0"], bufs["q1"], cos2, sin2],
                  [pl.BlockSpec((mt, D), row)] + [pl.BlockSpec((D, half), const)] * 2 + [tab, tab],
                  [sd((T, qw), BF), sd((T, kw), BF), sd((T, kw), BF)],
                  [pl.BlockSpec((mt, qw), row), pl.BlockSpec((mt, kw), row), pl.BlockSpec((mt, kw), row)],
                  [(0, [(WO, 2)] + acts(0))], flops=2 * T * D * qk, nbytes=4 * T * D)
    o = []
    for j in range(kv):
        cid += 1
        gw = qw // kv
        o += run("attn%d" % j, cid, functools.partial(attn_body, hd, 256, 4), (B,), [q, k, v],
                 [pl.BlockSpec((S, gw), lambda b, j=j: (b, j)), pl.BlockSpec((S, hd), lambda b, j=j: (b, j)), pl.BlockSpec((S, hd), lambda b, j=j: (b, j))],
                 [sd((T, gw), BF)], [pl.BlockSpec((S, gw), row)],
                 [(0, [(WO, 3 + j)] + acts(1 + j))], flops=T * S * gw * 8, nbytes=4 * T * gw)
    cid += 1
    x1, h2 = run("wout", cid, wout_body, (T // mt,), o + [bufs["wo"], x, gm],
                 [pl.BlockSpec((mt, qw // kv), row)] * kv + [pl.BlockSpec((qw, D), const), pl.BlockSpec((mt, D), row), pl.BlockSpec((1, D), const)],
                 [sd((T, D), BF)] * 2, [pl.BlockSpec((mt, D), row)] * 2, [(0, acts(3))], flops=2 * T * D * qw, nbytes=8 * T * D)
    r, n0 = None, 0
    mtg = 768
    for j, u in enumerate(GU_UNITS):
        cid += 1
        ins = [h2, bufs["g%d" % j], bufs["u%d" % j]] + ([r] if r is not None else [])
        specs = [pl.BlockSpec((mtg, D), lambda n, i: (i, 0)), pl.BlockSpec((D, UNIT), lambda n, i: (0, n)), pl.BlockSpec((D, UNIT), lambda n, i: (0, n))]
        specs += [pl.BlockSpec(memory_space=HBM)] if r is not None else []
        r, = run("gateup%d" % j, cid, functools.partial(gu_body, mtg), (u, T // mtg), ins, specs,
                 [sd((T, ff), BF)], [pl.BlockSpec((mtg, UNIT), lambda n, i, n0=n0: (i, n0 + n))],
                 [(0, acts(4 + j))], flops=4 * T * D * UNIT * u, nbytes=4 * T * D, alias={3: 0} if r is not None else None)
        n0 += u
    out, c0 = None, 0
    for j, w in enumerate(DOWN_COLS):
        cid += 1
        ins = [r, bufs["d%d" % j], x1] + ([out] if out is not None else [])
        off = c0 // w
        specs = [pl.BlockSpec((mt, ff), row), pl.BlockSpec((ff, w), const), pl.BlockSpec((mt, w), lambda i, off=off: (i, off))]
        specs += [pl.BlockSpec(memory_space=HBM)] if out is not None else []
        a = acts(4 + len(GU_UNITS) + j)
        out, = run("down%d" % j, cid, down_body, (T // mt,), ins, specs, [sd((T, D), BF)], [pl.BlockSpec((mt, w), lambda i, off=off: (i, off))],
                   [(0, a)] if a else [], flops=2 * T * ff * w, nbytes=2 * T * ff, alias={3: 0} if out is not None else None)
        c0 += w
    return out.reshape(B, S, D), k.reshape(B, S, kv, hd), v.reshape(B, S, kv, hd)


def solution(mesh):
    tok = P(("dp", "fsdp"), None, None)
    cache = P(("dp", "fsdp"), None, None, None)
    rowp, gain, table = P("fsdp", None), P("fsdp"), P(None, None)
    return jax.shard_map(functools.partial(local_layer, mesh.shape["fsdp"]), mesh=mesh,
                         in_specs=(tok, gain, rowp, rowp, rowp, rowp, gain, rowp, rowp, rowp, table, table),
                         out_specs=(tok, cache, cache), check_vma=False)
```

time: 894 us -> 747 us (0.84)
  Pallas kernels: 0 us -> 686 us
  matrix products: 521 us -> 0 us
  waiting for transfers between devices: 189 us -> 0 us
  other arithmetic: 71.9 us -> 4.62 us
  local copies, waits for them, and re-layouts: 45 us -> 20.7 us
  blocking collectives: 45.4 us -> 24.2 us
  between operations: 14.6 us -> 1.2 us
    pallas_call x0 -> x16, Pallas kernels: none -> 686 us  [call(): pl.pallas_call(kernel, grid=grid, in_specs=list(in_specs) + [hb] * (len(l...]
    dot_general x12 -> x0, matrix products: 501 us -> none  [the longest x1 137 us: decoder_layer(): jnp.dot(normed_mlp, w_gate, preferred_element_type=jnp.float32)]
    all_gather x7 -> x0, waiting for transfers between devices: 185 us -> none  [the longest x1 83.4 us: local_layer(): gather_rows(w_gate)]
    sub x2 -> x0, other arithmetic: 43.4 us -> none  [causal_attention(): prob_bf16 = jax.nn.softmax(scores, axis=-1).astype(jnp.bfloat16)]
    all_gather x2 -> x1, blocking collectives: 45.4 us -> 24.2 us  [local_layer(): lax.all_gather(jnp.stack([g_attn, g_mlp]), 'fsdp', axis=1, tiled=True)]
    sub x1 -> x0, matrix products: 20.2 us -> none  [causal_attention(): prob_bf16 = jax.nn.softmax(scores, axis=-1).astype(jnp.bfloat16)]
    another operation x2, local copies, waits for them, and re-layouts: 19.7 us -> 1.32 us  [local_layer(): jnp.stack([g_attn, g_mlp])]
    unnamed x45 -> x3, local copies, waits for them, and re-layouts: 25 us -> 11.5 us
  transfers between devices with their start and end apart: 7 -> 0, of which waited for: 4 -> 0; matrix products, arithmetic and copies ran while one was open for 58% -> 0% of each run, Pallas kernels for 0% -> 0%
where the time goes in v1:
time: 747 us; the launch traced here: 736 us
  Pallas kernels  686 us (92%)
  blocking collectives  24.2 us (3%)
  local copies, waits for them, and re-layouts  20.7 us (3%)
    pallas_call x16, Pallas kernels, call(): pl.pallas_call(kernel, grid=grid, in_specs=list(in_specs) + [hb] * (len(l...  686 us
    all_gather x1, blocking collectives, local_layer(): lax.all_gather(jnp.stack([g_attn, g_mlp]), 'fsdp', axis=1, tiled=True)  24.2 us

profile of v1, /device:TPU:112, one launch (start us, length us, event | category | flops | bytes accessed | tf_op | source)
XLA Modules:
  0.0 736.3 jit_solution(1166481482463307470)
XLA Ops:
  0.6 0.7 stack.9
  1.3 0.7 stack.10
  2.0 24.2 %all_gather.3 = bf16[2,2048]{1,0:T(2,128)(2,1)S(1)} all-gather(bf16[2,256]{1,0:T(2,128)(2,1)S(1)} %pad_maximum_fusion.3), channel_id=1, replica_groups=mesh['dp'=2,'fsdp'=8] {'fsdp'}, dimensions={1}, use_global_device_ids=true | all-gather | bytes 9216 | tf_op jit(solution)/shard_map/all_gather | solution.py:285
  26.2 0.6 fusion
  26.8 0.9 neg.3
  27.8 0.2 copy.87
  27.9 1.1 copy.85
  29.0 1.1 copy.88
  30.1 1.2 pad_maximum_fusion.1
  31.3 2.5 pad_maximum_fusion.refs_2_
  33.8 54.1 %gather_norm.1 = (bf16[2304,2048]{1,0:T(8,128)(2,1)}, bf16[2048,1280]{1,0:T(8,128)(2,1)}, bf16[2048,1280]{1,0:T(8,128)(2,1)}, bf16[2048,2048]{1,0:T(8,128)(2,1)}) custom-call(bf16[2304,2048]{1,0:T(8,128)(2,1)} %bitcast.2, bf16[1,2048]{1,0:T(2,128)(2,1)} %get-tuple-element.196.refs_1_, bf16[256,2560]{1,0:T(8,128)(2,1)} %pad_maximum_fusion.refs_2_, ...), custom_call_target="tpu_custom_call" | custom-call | tf_op jit(solution)/shard_map/gather_norm/pallas_call | solution.py:156
  87.9 40.7 %qkv.1 = (bf16[2304,2048]{1,0:T(8,128)(2,1)}, bf16[2304,256]{1,0:T(8,128)(2,1)}, bf16[2304,256]{1,0:T(8,128)(2,1)}, bf16[2048,2048]{1,0:T(8,128)(2,1)}, bf16[204...) custom-call(bf16[2304,2048]{1,0:T(8,128)(2,1)} %get-tuple-element.99.refs_0_, ...), custom_call_target="tpu_custom_call", output_to_operand_aliasing={{3}: (7, {})} | custom-call | flops 24159191040 | bytes 18874368 | tf_op jit(solution)/shard_map/qkv/pallas_call | solution.py:156
  128.5 3.5 reshape.20
  132.1 3.5 reshape.21
  135.6 39.3 %attn0.1 = (bf16[2304,1024]{1,0:T(8,128)(2,1)}, bf16[2048,2048]{1,0:T(8,128)(2,1)}, bf16[2048,1536]{1,0:T(8,128)(2,1)}, bf16[2048,1536]{1,0:T(8,128)(2,1)}, bf16...) custom-call(bf16[2304,2048]{1,0:T(8,128)(2,1)} %get-tuple-element.10, ...), custom_call_target="tpu_custom_call", output_to_operand_aliasing={{1}: (5, {}), {2}: (6, {}), {3}: (7, {})} | custom-call | flops 14495514624 | bytes 9437184 | tf_op jit(solution)/shard_map/attn0/pallas_call | solution.py:156
  174.9 40.7 %attn1.1 = (bf16[2304,1024]{1,0:T(8,128)(2,1)}, bf16[2048,2048]{1,0:T(8,128)(2,1)}, bf16[2048,1536]{1,0:T(8,128)(2,1)}, bf16[2048,1536]{1,0:T(8,128)(2,1)}, bf16...) custom-call(bf16[2304,2048]{1,0:T(8,128)(2,1)} %get-tuple-element.10, ...), custom_call_target="tpu_custom_call", output_to_operand_aliasing={{1}: (5, {}), {2}: (6, {}), {3}: (7, {}), {4}: (8, {}), {5}... | custom-call | flops 14495514624 | bytes 9437184 | tf_op jit(solution)/shard_map/attn1/pallas_call | solution.py:156
  215.6 42.7 %wout.1 = (bf16[2304,2048]{1,0:T(8,128)(2,1)}, bf16[2304,2048]{1,0:T(8,128)(2,1)}, bf16[2048,1536]{1,0:T(8,128)(2,1)}, bf16[2048,1536]{1,0:T(8,128)(2,1)}, bf16[...) custom-call(bf16[2304,1024]{1,0:T(8,128)(2,1)} %get-tuple-element.10, ...), custom_call_target="tpu_custom_call", output_to_operand_aliasing={{2}: (7, {}), {3}: (8, {}), {4}: (9, {}), {5}: (10, {}), {6... | custom-call | flops 19327352832 | bytes 37748736 | tf_op jit(solution)/shard_map/wout/pallas_call | solution.py:156
  258.3 45.3 %gateup0.1 = (bf16[2304,11008]{1,0:T(8,128)(2,1)}, bf16[2048,1536]{1,0:T(8,128)(2,1)}, bf16[2048,1536]{1,0:T(8,128)(2,1)}, bf16[2048,1536]{1,0:T(8,128)(2,1)}, b...) custom-call(bf16[2304,2048]{1,0:T(8,128)(2,1)} %get-tuple-element.12, ...), custom_call_target="tpu_custom_call", output_to_operand_aliasing={{1}: (5, {}), {2}: (6, {}), {3}: (7, {}), {4}: (8, {}), {5}... | custom-call | flops 28991029248 | bytes 18874368 | tf_op jit(solution)/shard_map/gateup0/pallas_call | solution.py:156
  303.6 45.0 %gateup1.1 = (bf16[2304,11008]{1,0:T(8,128)(2,1)}, bf16[2048,1536]{1,0:T(8,128)(2,1)}, bf16[2048,1536]{1,0:T(8,128)(2,1)}, bf16[2048,1536]{1,0:T(8,128)(2,1)}, b...) custom-call(bf16[2304,2048]{1,0:T(8,128)(2,1)} %get-tuple-element.12, ...), custom_call_target="tpu_custom_call", output_to_operand_aliasing={{0}: (3, {}), {1}: (6, {}), {2}: (7, {}), {3}: (8, {}), {4}... | custom-call | flops 28991029248 | bytes 18874368 | tf_op jit(solution)/shard_map/gateup1/pallas_call | solution.py:156
  348.6 45.6 %gateup2.1 = (bf16[2304,11008]{1,0:T(8,128)(2,1)}, bf16[2048,1536]{1,0:T(8,128)(2,1)}, bf16[2048,1536]{1,0:T(8,128)(2,1)}, bf16[2048,1536]{1,0:T(8,128)(2,1)}, b...) custom-call(bf16[2304,2048]{1,0:T(8,128)(2,1)} %get-tuple-element.12, ...), custom_call_target="tpu_custom_call", output_to_operand_aliasing={{0}: (3, {}), {1}: (6, {}), {2}: (7, {}), {3}: (8, {}), {4}... | custom-call | flops 28991029248 | bytes 18874368 | tf_op jit(solution)/shard_map/gateup2/pallas_call | solution.py:156
  394.2 45.9 %gateup3.1 = (bf16[2304,11008]{1,0:T(8,128)(2,1)}, bf16[2048,1792]{1,0:T(8,128)(2,1)}, bf16[2048,1792]{1,0:T(8,128)(2,1)}, bf16[2048,1536]{1,0:T(8,128)(2,1)}, b...) custom-call(bf16[2304,2048]{1,0:T(8,128)(2,1)} %get-tuple-element.12, ...), custom_call_target="tpu_custom_call", output_to_operand_aliasing={{0}: (3, {}), {1}: (5, {}), {2}: (6, {}), {3}: (7, {}), {4}... | custom-call | flops 28991029248 | bytes 18874368 | tf_op jit(solution)/shard_map/gateup3/pallas_call | solution.py:156
  440.1 44.7 %gateup4.1 = (bf16[2304,11008]{1,0:T(8,128)(2,1)}, bf16[11008,512]{1,0:T(8,128)(2,1)}, bf16[2048,1792]{1,0:T(8,128)(2,1)}, bf16[2048,1792]{1,0:T(8,128)(2,1)}, b...) custom-call(bf16[2304,2048]{1,0:T(8,128)(2,1)} %get-tuple-element.12, ...), custom_call_target="tpu_custom_call", output_to_operand_aliasing={{0}: (3, {}), {1}: (5, {}), {2}: (6, {}), {3}: (7, {}), {4}... | custom-call | flops 28991029248 | bytes 18874368 | tf_op jit(solution)/shard_map/gateup4/pallas_call | solution.py:156
  484.8 44.2 %gateup5.1 = (bf16[2304,11008]{1,0:T(8,128)(2,1)}, bf16[11008,512]{1,0:T(8,128)(2,1)}, bf16[11008,512]{1,0:T(8,128)(2,1)}, bf16[2048,1792]{1,0:T(8,128)(2,1)}, b...) custom-call(bf16[2304,2048]{1,0:T(8,128)(2,1)} %get-tuple-element.12, ...), custom_call_target="tpu_custom_call", output_to_operand_aliasing={{0}: (3, {}), {1}: (5, {}), {2}: (6, {}), {3}: (7, {}), {4}... | custom-call | flops 28991029248 | bytes 18874368 | tf_op jit(solution)/shard_map/gateup5/pallas_call | solution.py:156
  529.0 51.1 %gateup6.1 = (bf16[2304,11008]{1,0:T(8,128)(2,1)}, bf16[11008,512]{1,0:T(8,128)(2,1)}, bf16[11008,512]{1,0:T(8,128)(2,1)}, bf16[11008,512]{1,0:T(8,128)(2,1)}, bf16[11008,512]{1,0:T(8,128)(2,1)}) custom-call(bf16[2304,2048]{1,0:T(8,128)(2,1)} %get-tuple-element.123.refs_0_, ...), custom_call_target="tpu_custom_call", output_to_operand_aliasing={{0}: (3, {}), {1}: (5, {}), {2}: (6, {}), {3}: (7, {})} | custom-call | flops 33822867456 | bytes 18874368 | tf_op jit(solution)/shard_map/gateup6/pallas_call | solution.py:156
  580.1 36.9 %down0.1 = (bf16[2304,2048]{1,0:T(8,128)(2,1)}, bf16[11008,512]{1,0:T(8,128)(2,1)}, bf16[11008,512]{1,0:T(8,128)(2,1)}, bf16[11008,512]{1,0:T(8,128)(2,1)}) custom-call(bf16[2304,11008]{1,0:T(8,128)(2,1)} %get-tuple-element.180.refs_0_, bf16[11008,512]{1,0:T(8,128)(2,1)} %get-tuple-element.181.refs_1_, ...), custom_call_target="tpu_custom_call", output_to_operand_aliasing={{1}: (3, {}), {2}: (4, {}), {3}: (5, {})} | custom-call | flops 25971130368 | bytes 50724864 | tf_op jit(solution)/shard_map/down0/pallas_call | solution.py:156
  617.0 37.1 %down1.1 = (bf16[2304,2048]{1,0:T(8,128)(2,1)}, bf16[11008,512]{1,0:T(8,128)(2,1)}, bf16[11008,512]{1,0:T(8,128)(2,1)}) custom-call(bf16[2304,11008]{1,0:T(8,128)(2,1)} %get-tuple-element.180.refs_0_, bf16[11008,512]{1,0:T(8,128)(2,1)} %get-tuple-element.186.refs_1_, ...), custom_call_target="tpu_custom_call", output_to_operand_aliasing={{0}: (3, {}), {1}: (4, {}), {2}: (5, {})} | custom-call | flops 25971130368 | bytes 50724864 | tf_op jit(solution)/shard_map/down1/pallas_call | solution.py:156
  654.1 36.3 %down2.1 = (bf16[2304,2048]{1,0:T(8,128)(2,1)}, bf16[11008,512]{1,0:T(8,128)(2,1)}) custom-call(bf16[2304,11008]{1,0:T(8,128)(2,1)} %get-tuple-element.180.refs_0_, bf16[11008,512]{1,0:T(8,128)(2,1)} %get-tuple-element.190.refs_1_, bf16[2304,2048]{1,0:T(8,128)(2,1)} %get-tuple-element.182.refs_2_, ...), custom_call_target="tpu_custom_call", output_to_operand_aliasing={{0}: (3, {}), {1}: (4, {})} | custom-call | flops 25971130368 | bytes 50724864 | tf_op jit(solution)/shard_map/down2/pallas_call | solution.py:156
  690.4 36.1 %down3.1 = bf16[2304,2048]{1,0:T(8,128)(2,1)} custom-call(bf16[2304,11008]{1,0:T(8,128)(2,1)} %get-tuple-element.180.refs_0_, bf16[11008,512]{1,0:T(8,128)(2,1)} %get-tuple-element.193.refs_1_, bf16[2304,2048]{1,0:T(8,128)(2,1)} %get-tuple-element.182.refs_2_, bf16[2304,2048]{1,0:T(8,128)(2,1)} %get-tuple-element.194.refs_3_), custom_call_target="tpu_custom_call", output_to_operand_aliasing={{}: (3, {})} | custom-call | flops 25971130368 | bytes 50724864 | tf_op jit(solution)/shard_map/down3/pallas_call | solution.py:156
  726.5 9.4 %copy.156 = bf16[3,768,2048]{2,1,0:T(8,128)(2,1)} copy(bf16[3,768,2048]{2,1,0:T(8,128)(2,1)} %bitcast.4) | data formatting | bytes 18874368
  (1 shorter events, 0.0 us)

commit v2 on v1

v2 whole, which is shorter than its diff:
```python
import functools, math
import jax, jax.numpy as jnp
from jax import lax
from jax.experimental import pallas as pl
from jax.experimental.pallas import tpu as pltpu
from jax.sharding import PartitionSpec as P

F32 = jnp.float32
BF = jnp.bfloat16
MESH = pl.DeviceIdType.MESH
HBM = pltpu.MemorySpace.HBM
EPS = 1e-5


class Group:
    def __init__(self, name, local, col0, outer, common, rows, nblk):
        self.name, self.local, self.col0 = name, local, col0
        self.outer, self.common, self.rows, self.nblk = outer, common, rows, nblk
        self.width = 2 * outer + common

    def shape(self):
        return jax.ShapeDtypeStruct((self.rows * self.nblk, self.width), BF)


def place(nblk):
    me = lax.axis_index("fsdp")
    dp = lax.axis_index("dp")
    core = lax.rem(me, 2)
    chip = me // 2
    chips = nblk // 2
    par = lax.rem(dp, 2)
    blk = lambda k: lax.rem(chip + k, chips) * 2 + core
    return dict(me=me, dp=dp, par=par, core=core,
                left=blk(chips - 1), right=blk(1), far=blk(2), mate=me + 1 - 2 * core,
                dev_left=(dp, blk(chips - 1)), dev_right=(dp, blk(1)), dev_mate=(dp, me + 1 - 2 * core),
                dev_pair=(dp + 1 - 2 * par, me))


def stage_copies(g, stage, at, loc, full):
    R, H, m, mc = g.rows, g.rows // 2, g.outer, g.outer + g.common
    par = at["par"]
    cols = lambda start, n: pl.ds(pl.multiple_of(start, 128), n)
    rows = lambda b, o=0, n=R: pl.ds(pl.multiple_of(b * R + o, 16), n)
    xr, mine, theirs = cols(par * m, mc), cols(par * mc, m), cols((1 - par) * mc, m)
    if stage == 1:
        src = loc.at[:, cols(g.col0 + par * m, mc)]
        own = rows(at["me"])
        return [(src, full.at[own, xr], at["dev_right"]), (src, full.at[own, xr], at["dev_left"]),
                (loc.at[:, pl.ds(g.col0, g.width)], full.at[own, :], at["dev_mate"])]
    same = lambda r, c, dev: (full.at[r, c], full.at[r, c], dev)
    lo, hi, far, mate = at["left"], at["right"], at["far"], at["mate"]
    allc = pl.ds(0, g.width)
    if stage == 2:
        out = [same(rows(lo, 0, H), xr, at["dev_right"]), same(rows(hi, H, H), xr, at["dev_left"])]
        if m:
            out += [same(rows(lo), mine, at["dev_pair"]), same(rows(hi), mine, at["dev_pair"])]
        return out + [same(rows(lo), xr, at["dev_mate"]), same(rows(hi), xr, at["dev_mate"]), same(rows(mate), allc, at["dev_mate"])]
    if stage == 3:
        out = []
        if m:
            out += [same(rows(far), mine, at["dev_pair"])]
        out += [same(rows(far), xr, at["dev_mate"])]
        if m:
            out += [same(rows(lo), theirs, at["dev_mate"]), same(rows(hi), theirs, at["dev_mate"])]
        return out
    return [same(rows(far), theirs, at["dev_mate"])] if m else []


def n_copies(g, stage):
    m = g.outer > 0
    return {1: 3, 2: 7 if m else 5, 3: 4 if m else 1, 4: 1 if m else 0}[stage]


def call(name, cid, body, grid, ins, in_specs, outs, out_specs, ticks, bufs, locs, nblk, flops=0, nbytes=0, scratch=(), alias=None, pre=None, everyone=False, held=()):
    groups = []
    for _, acts in ticks:
        for g, s in acts:
            if g not in groups:
                groups.append(g)
    old = [g for g in groups if g.name in bufs]
    new = [g for g in groups if g.name not in bufs]
    lnames = []
    for _, acts in ticks:
        for g, s in acts:
            if s == 1 and g.local not in lnames:
                lnames.append(g.local)
    base, total = {}, 0
    for _, acts in ticks:
        for g, s in acts:
            base[(g.name, s)] = total
            total += n_copies(g, s)
    nsteps = math.prod(grid)
    n_in, n_out, n_sc = len(ins), len(outs), len(scratch)
    in_specs = [pl.BlockSpec(memory_space=HBM) if k in held else sp for k, sp in enumerate(in_specs)]

    def kernel(*refs):
        cin, refs = refs[:n_in], refs[n_in:]
        lrefs, refs = refs[:len(lnames)], refs[len(lnames):]
        refs = refs[len(old):]
        couts, refs = refs[:n_out], refs[n_out:]
        gref, refs = refs[:len(groups)], refs[len(groups):]
        sc, refs = refs[:n_sc], refs[n_sc:]
        step = pl.program_id(0)
        for k in range(1, len(grid)):
            step = step * grid[k] + pl.program_id(k)
        if held:
            kept, hsem, refs = refs[:len(held)], refs[len(held)], refs[len(held) + 1:]
            loads = [pltpu.make_async_copy(cin[k], b, hsem.at[i]) for i, (k, b) in enumerate(zip(held, kept))]
            cin = list(cin)
            for k, b in zip(held, kept):
                cin[k] = b

            @pl.when(step == 0)
            def _():
                for cp in loads:
                    cp.start()

        def compute():
            if held:
                @pl.when(step == 0)
                def _():
                    for cp in loads:
                        cp.wait()
            body(cin, couts, sc)

        if not total:
            compute()
            return
        ssem, rsem = refs
        full = {g.name: r for g, r in zip(old + new, gref)}
        loc = dict(zip(lnames, lrefs))
        at = place(nblk)
        if pre is not None:
            pre(step, cin, sc)

        def copies(g, s):
            b = base[(g.name, s)]
            return [pltpu.make_async_remote_copy(src_ref=a, dst_ref=d, send_sem=ssem.at[b + k], recv_sem=rsem.at[b + k],
                                                 device_id=dev, device_id_type=MESH)
                    for k, (a, d, dev) in enumerate(stage_copies(g, s, at, loc.get(g.local), full[g.name]))]

        got = set()
        for n, (when, acts) in enumerate(ticks):
            need = []
            for g, s in acts:
                if (g.name, s - 1) in base and (g.name, s - 1) not in got:
                    need.append((g, s - 1))
                    got.add((g.name, s - 1))

            @pl.when(step == when)
            def _():
                if n == 0:
                    bar = pltpu.get_barrier_semaphore()
                    peers = [at[dev] for dev in ("dev_left", "dev_right", "dev_mate", "dev_pair")]
                    if everyone:
                        peers = [(at["dp"], lax.rem(at["me"] + j, nblk)) for j in range(1, nblk)] + [at["dev_pair"]]
                    for dev in peers:
                        pl.semaphore_signal(bar, inc=1, device_id=dev, device_id_type=MESH)
                    pl.semaphore_wait(bar, len(peers))
                for g, s in need:
                    for cp in copies(g, s):
                        cp.wait_recv()
                for g, s in acts:
                    for cp in copies(g, s):
                        cp.start()

        compute()

        @pl.when(step == nsteps - 1)
        def _():
            for _, acts in ticks:
                for g, s in acts:
                    for cp in copies(g, s):
                        if (g.name, s) not in got:
                            cp.wait_recv()
                        cp.wait_send()

    hb = pl.BlockSpec(memory_space=HBM)
    al = dict(alias or {})
    for k in range(len(old)):
        al[n_in + len(lnames) + k] = n_out + k
    res = pl.pallas_call(
        kernel, grid=grid,
        in_specs=list(in_specs) + [hb] * (len(lnames) + len(old)),
        out_specs=list(out_specs) + [hb] * len(groups),
        out_shape=list(outs) + [g.shape() for g in old + new],
        scratch_shapes=list(scratch) + ([pltpu.VMEM(ins[k].shape, ins[k].dtype) for k in held] + [pltpu.SemaphoreType.DMA((len(held),))] if held else []) + ([pltpu.SemaphoreType.DMA((total,)), pltpu.SemaphoreType.DMA((total,))] if total else []),
        input_output_aliases=al,
        compiler_params=pltpu.CompilerParams(vmem_limit_bytes=62 << 20, **(dict(collective_id=cid, has_side_effects=True) if total else {})),
        cost_estimate=pl.CostEstimate(flops=flops, bytes_accessed=nbytes, transcendentals=0),
        name=name)(*ins, *[locs[n] for n in lnames], *[bufs[g.name] for g in old])
    for g, b in zip(old + new, res[n_out:]):
        bufs[g.name] = b
    return res[:n_out]


GROWS = 16


def norm_body(nblk, skip, cin, couts, sc):
    x_ref, gl_ref = cin
    h_ref, gm_ref = couts
    gbuf, ga, ssem, rsem, osem = sc
    step = pl.program_id(0)
    me, dp = lax.axis_index("fsdp"), lax.axis_index("dp")
    mine = gbuf.at[pl.ds(pl.multiple_of(me * GROWS, GROWS), GROWS), :]
    sends = [pltpu.make_async_remote_copy(src_ref=gl_ref, dst_ref=mine, send_sem=ssem.at[j - 1], recv_sem=rsem.at[j - 1],
                                          device_id=(dp, lax.rem(me + j, nblk)), device_id_type=MESH) for j in range(1, nblk)]
    own = pltpu.make_async_copy(gl_ref, mine, osem.at[0])

    @pl.when(step == 0)
    def _():
        own.start()
        for cp in sends:
            cp.start()

    row = lambda k: jnp.concatenate([gbuf[b * GROWS + k:b * GROWS + k + 1, :] for b in range(nblk)], axis=1)

    @pl.when(step == skip)
    def _():
        own.wait()
        for cp in sends:
            cp.wait()
        gm_ref[...] = row(1)
        ga[...] = row(0).astype(F32)

    @pl.when(jnp.logical_and(step >= skip, step < pl.num_programs(0) - 1))
    def _():
        def rows(k, _):
            rs = pl.ds(pl.multiple_of(k * GROWS, GROWS), GROWS)
            x = x_ref[rs, :].astype(F32)
            r = lax.rsqrt(jnp.mean(x * x, axis=-1, keepdims=True) + EPS)
            h_ref[rs, :] = (x * r * ga[...]).astype(BF)
            return 0
        lax.fori_loop(0, x_ref.shape[0] // GROWS, rows, 0, unroll=4)


def proj_body(roped, cin, couts, sc):
    h_ref, w_refs, (cos_ref, sin_ref) = cin[0], cin[1:1 + len(roped)], cin[1 + len(roped):3 + len(roped)]
    hd = 2 * cos_ref.shape[1]
    c = jnp.concatenate([cos_ref[...], cos_ref[...]], axis=1)
    s = jnp.concatenate([-sin_ref[...], sin_ref[...]], axis=1)
    for w_ref, out_ref, rope in zip(w_refs, couts, roped):
        for n0 in range(0, w_ref.shape[1], 2 * hd):
            acc = jnp.dot(h_ref[...], w_ref[:, n0:n0 + 2 * hd], preferred_element_type=F32).astype(BF)
            for j in (0, hd):
                part = acc[:, j:j + hd]
                if rope:
                    t = part.astype(F32)
                    part = (t * c + pltpu.roll(t, hd // 2, 1) * s).astype(BF)
                out_ref[:, n0 + j:n0 + j + hd] = part


def attn_body(hd, qb, unroll, cin, couts, sc):
    q_ref, k_ref, v_ref = cin[:3]
    o_ref = couts[0]

    @pl.when(pl.program_id(0) == 0)
    def _():
        for src, dst in zip(cin[3:], couts[1:]):
            for j in range(dst.shape[1]):
                dst[:, j, :] = src[:, j * hd:(j + 1) * hd]
    S, nh = q_ref.shape[0], q_ref.shape[1] // hd
    scale = hd ** -0.5 * math.log2(math.e)
    mask = lax.broadcasted_iota(jnp.int32, (qb, qb), 0) >= lax.broadcasted_iota(jnp.int32, (qb, qb), 1)

    for b in range(S // qb):
        r0, n = b * qb, (b + 1) * qb

        def step(i, _):
            heads = [pl.ds(pl.multiple_of((i * unroll + u) * hd, hd), hd) for u in range(unroll)]
            scores = [lax.dot_general(q_ref[r0:n, hs], k_ref[:n, :], (((1,), (1,)), ((), ())), preferred_element_type=F32) for hs in heads]
            for hs, s in zip(heads, scores):
                diag = jnp.where(mask, s[:, r0:], -jnp.inf)
                s = diag if r0 == 0 else jnp.concatenate([s[:, :r0], diag], axis=1)
                p = jnp.exp2((s - jnp.max(s, axis=1, keepdims=True)) * scale)
                pb = (p * (1.0 / jnp.sum(p, axis=1, keepdims=True))).astype(BF)
                o_ref[r0:n, hs] = jnp.dot(pb, v_ref[:n, :], preferred_element_type=F32).astype(BF)
            return 0
        lax.fori_loop(0, nh // unroll, step, 0)


def wout_body(cin, couts, sc):
    o_ref, w_ref, x_ref, g_ref = cin
    x1_ref, h_ref = couts
    D = w_ref.shape[1]
    o = o_ref[...]
    ss = jnp.zeros((o.shape[0], 1), F32)
    step = min(512, D)
    for n0 in range(0, D, step):
        cs = slice(n0, n0 + step)
        a = jnp.dot(o, w_ref[:, cs], preferred_element_type=F32).astype(BF)
        x1 = (x_ref[:, cs].astype(F32) + a.astype(F32)).astype(BF)
        x1_ref[:, cs] = x1
        xf = x1.astype(F32)
        ss = ss + jnp.sum(xf * xf, axis=1, keepdims=True)
    r = lax.rsqrt(ss / D + EPS)
    for n0 in range(0, D, step):
        cs = slice(n0, n0 + step)
        h_ref[:, cs] = (x1_ref[:, cs].astype(F32) * r * g_ref[:, cs].astype(F32)).astype(BF)


def gu_loads(mt, cin, sc):
    hbuf, sem = sc
    return [pltpu.make_async_copy(cin[0].at[pl.ds(k * mt, mt), :], hbuf.at[pl.ds(k * mt, mt), :], sem.at[k]) for k in range(hbuf.shape[0] // mt)]


def gu_pre(mt, step, cin, sc):
    @pl.when(step == 0)
    def _():
        for cp in gu_loads(mt, cin, sc):
            cp.start()


def gu_body(mt, cin, couts, sc):
    wg_ref, wu_ref = cin[1:3]
    r_ref, = couts
    hbuf = sc[0]

    def rows(k, _):
        rs = pl.ds(pl.multiple_of(k * mt, mt), mt)

        @pl.when(pl.program_id(0) == 0)
        def _():
            pltpu.make_async_copy(cin[0].at[rs, :], hbuf.at[rs, :], sc[1].at[k]).wait()
        hh = hbuf[rs, :]
        g = jnp.dot(hh, wg_ref[...], preferred_element_type=F32).astype(BF).astype(F32)
        u = jnp.dot(hh, wu_ref[...], preferred_element_type=F32).astype(BF).astype(F32)
        r_ref[rs, :] = ((g / (1.0 + jnp.exp(-g))) * u).astype(BF)
        return 0
    lax.fori_loop(0, hbuf.shape[0] // mt, rows, 0)


def down_tiles(c0, r_ref, w_ref, x_ref, out_ref):
    m = jnp.dot(r_ref[...], w_ref[...], preferred_element_type=F32).astype(BF)
    out_ref[:, c0:c0 + w_ref.shape[1]] = (x_ref[...].astype(F32) + m.astype(F32)).astype(BF)


def down_loop(c0, r_ref, w_ref, x_ref, out_ref):
    def tile(n, _):
        cs = pl.ds(pl.multiple_of(n * UNIT, UNIT), UNIT)
        m = jnp.dot(r_ref[...], w_ref[:, cs], preferred_element_type=F32).astype(BF)
        out_ref[:, pl.ds(pl.multiple_of(c0 + n * UNIT, UNIT), UNIT)] = (x_ref[:, cs].astype(F32) + m.astype(F32)).astype(BF)
        return 0
    lax.fori_loop(0, w_ref.shape[1] // UNIT, tile, 0)


def down_body(cin, couts, sc):
    down_tiles(0, *cin, couts[0])


def down_loop_body(cin, couts, sc):
    down_loop(0, *cin, couts[0])


def last_body(cin, couts, sc):
    r_ref, w_ref, x_ref, *parts = cin
    out_ref, = couts
    c0 = 0
    for p in parts:
        out_ref[:, c0:c0 + p.shape[1]] = p[...]
        c0 += p.shape[1]
    down_tiles(c0, r_ref, w_ref, x_ref, out_ref)


UNIT = 256
GU_UNITS = (6, 6, 6, 6, 6, 6, 7)
DOWN_COLS = (512, 512, 512, 512)


def thirds(cols, unit, frac=1 / 3):
    outer = int(cols // unit * frac + 0.5) * unit
    return outer, cols - 2 * outer


def local_layer(nblk, hidden, g_attn, w_query, w_key, w_value, w_out, g_mlp, w_gate, w_up, w_down, cos_tab, sin_tab):
    B, S, D = hidden.shape
    T = B * S
    hd = 2 * cos_tab.shape[1]
    qw, kw = w_query.shape[1], w_key.shape[1]
    ff = w_gate.shape[1]
    kv = kw // hd
    x = hidden.reshape(T, D)
    gl = jnp.pad(jnp.stack([g_attn, g_mlp]), ((0, GROWS - 2), (0, 0)))
    locs = dict(wq=w_query, wk=w_key, wv=w_value, wo=w_out, wg=w_gate, wu=w_up, wd=w_down)
    rw = w_query.shape[0]
    qk = qw + 2 * kw
    half = qw // 2
    Q0 = [Group("q0", "wq", 0, 0, half, rw, nblk), Group("k", "wk", 0, 0, kw, rw, nblk), Group("v", "wv", 0, 0, kw, rw, nblk)]
    Q1 = [Group("q1", "wq", half, 0, half, rw, nblk)]
    WO = Group("wo", "wo", 0, *thirds(D, 128), rw, nblk)
    G, c0 = [], 0
    for k, u in enumerate(GU_UNITS):
        G.append([Group("g%d" % k, "wg", c0, *thirds(u * UNIT, 128), rw, nblk), Group("u%d" % k, "wu", c0, *thirds(u * UNIT, 128), rw, nblk)])
        c0 += u * UNIT
    assert c0 == ff
    Dn, c0 = [], 0
    for k, w in enumerate(DOWN_COLS):
        Dn.append(Group("d%d" % k, "wd", c0, *thirds(w, 128), w_down.shape[0], nblk))
        c0 += w
    assert c0 == D
    seq = [[g] if isinstance(g, Group) else g for g in G + Dn]

    def acts(i, late, extra=(), more=()):
        now = [(gs, s) for gs, s in extra]
        for s in (3, 2, 1):
            now += [(gs, s) for j, gs in enumerate(seq) if j + 2 + s - 1 == i]
        first = [(g, s) for gs, s in now for g in gs]
        then = list(more) + [(g, 4) for g, s in first if s == 3 and n_copies(g, 4)]
        return ([(0, first)] if first else []) + ([(late, then)] if then else [])

    bufs = {}
    run = functools.partial(call, bufs=bufs, locs=locs, nblk=nblk)
    sd = jax.ShapeDtypeStruct
    mt = 256
    row = lambda i: (i, 0)
    const = lambda *a: (0, 0)
    cid = 0
    skip, nrow = 1, T // mt
    last = nrow + skip - 1
    on = lambda gs, st: [(g, st) for g in gs if n_copies(g, st)]
    dma = pltpu.SemaphoreType.DMA
    rowk = lambda i: (jnp.clip(i - skip, 0, nrow - 1), 0)
    h, gm = run("gather_norm", cid, functools.partial(norm_body, nblk, skip), (nrow + skip + 1,), [x, gl],
                [pl.BlockSpec((mt, D), rowk), pl.BlockSpec(memory_space=HBM)],
                [sd((T, D), BF), sd((1, D), BF)], [pl.BlockSpec((mt, D), rowk), pl.BlockSpec((1, D), const)],
                [(0, on(Q0, 1)), (skip, on(Q0, 2) + on(Q1, 1)), (last + 1, on(Q0, 3))],
                scratch=[pltpu.VMEM((nblk * GROWS, gl.shape[1]), BF), pltpu.VMEM((1, D), F32), dma((nblk - 1,)), dma((nblk - 1,)), dma((1,))], everyone=True)
    tab = pl.BlockSpec((mt, hd // 2), lambda i: (i % (S // mt), 0))
    gw = qw // kv
    nt = T // mt
    wspec = lambda n: pl.BlockSpec((D, n), const)
    late = nt * 2 // 3

    def project(name, slot, ws, outs, specs, roped, extra, more=(), into=()):
        width = sum(bufs[w].shape[1] for w in ws)
        return run(name, cid, functools.partial(proj_body, roped), (nt,), [h] + [bufs[w] for w in ws] + [cos_tab, sin_tab] + list(into),
                   [pl.BlockSpec((mt, D), row)] + [wspec(bufs[w].shape[1]) for w in ws] + [tab, tab] + [pl.BlockSpec(memory_space=HBM)] * len(into),
                   outs, specs, acts(slot, late, extra, more), flops=2 * T * D * width, nbytes=4 * T * D,
                   held=tuple(range(1, 1 + len(ws))), alias={3 + len(ws): 0} if into else None)

    cid += 1
    q, k, v = project("proj0", 0, ["q0", "k", "v"], [sd((T, qw), BF), sd((T, kw), BF), sd((T, kw), BF)],
                      [pl.BlockSpec((mt, half), row), pl.BlockSpec((mt, kw), row), pl.BlockSpec((mt, kw), row)], (True, True, False),
                      [(Q1, 2), ([WO], 1)], [(Q1[0], 3)])
    cid += 1
    q, = project("proj1", 1, ["q1"], [sd((T, qw), BF)], [pl.BlockSpec((mt, half), lambda i: (i, 1))], (True,), [([WO], 2)], into=[q])
    cid += 1
    one = pl.BlockSpec((S, hd), lambda j, b: (b, j))
    grp = pl.BlockSpec((S, gw), lambda j, b: (b, j))
    whole = pl.BlockSpec((S, kw), lambda j, b: (jnp.where(j == 0, b, B - 1), 0))
    cube = pl.BlockSpec((S, kv, hd), lambda j, b: (jnp.where(j == 0, b, B - 1), 0, 0))
    ahead = [a for a in acts(3, 0)[0][1] if a[1] == 1]
    o, kc, vc = run("attn", cid, functools.partial(attn_body, hd, 256, 2), (kv, B), [q, k, v, k, v], [grp, one, one, whole, whole],
                    [sd((T, qw), BF)] + [sd((T, kv, hd), BF)] * 2, [grp, cube, cube],
                    [(0, acts(2, 0, [([WO], 3)])[0][1] + ahead), (kv * B // 2, [a for a in acts(3, 0)[0][1] if a not in ahead] + [(WO, 4)])], flops=T * S * qw * 8, nbytes=4 * T * qw)
    cid += 1
    x1, h2 = run("wout", cid, wout_body, (nt,), [o, bufs["wo"], x, gm],
                 [pl.BlockSpec((mt, qw), row), pl.BlockSpec((qw, D), const), pl.BlockSpec((mt, D), row), pl.BlockSpec((1, D), const)],
                 [sd((T, D), BF)] * 2, [pl.BlockSpec((mt, D), row)] * 2, acts(4, late), flops=2 * T * D * qw, nbytes=8 * T * D, held=(1,))
    r, n0 = None, 0
    mtg = S
    for j, u in enumerate(GU_UNITS):
        cid += 1
        hb = pl.BlockSpec(memory_space=HBM)
        ins = [h2, bufs["g%d" % j], bufs["u%d" % j]] + ([r] if r is not None else [])
        specs = [hb, pl.BlockSpec((D, UNIT), lambda n: (0, n)), pl.BlockSpec((D, UNIT), lambda n: (0, n))] + ([hb] if r is not None else [])
        r, = run("gateup%d" % j, cid, functools.partial(gu_body, mtg), (u,), ins, specs,
                 [sd((T, ff), BF)], [pl.BlockSpec((T, UNIT), lambda n, n0=n0: (0, n0 + n))],
                 acts(5 + j, u * 2 // 3), flops=4 * T * D * UNIT * u, nbytes=4 * T * D, alias={3: 0} if r is not None else None,
                 scratch=[pltpu.VMEM((T, D), BF), dma((T // mtg,))], pre=functools.partial(gu_pre, mtg))
        n0 += u
    parts, c0 = [], 0
    for j, w in enumerate(DOWN_COLS):
        cid += 1
        off = c0 // w
        ins = [r, bufs["d%d" % j], x1]
        specs = [pl.BlockSpec((mt, ff), row), pl.BlockSpec((ff, w), const), pl.BlockSpec((mt, w), lambda i, off=off: (i, off))]
        a = acts(5 + len(GU_UNITS) + j, late)
        cost = dict(flops=2 * T * ff * w, nbytes=2 * T * ff, held=(1,))
        if j < len(DOWN_COLS) - 1:
            parts += run("down%d" % j, cid, down_loop_body if j == 0 else down_body, (T // mt,), ins, specs, [sd((T, w), BF)], [pl.BlockSpec((mt, w), row)], a, **cost)
        else:
            assert not a
            out, = run("down%d" % j, cid, last_body, (T // mt,), ins + parts, specs + [pl.BlockSpec((mt, p.shape[1]), row) for p in parts],
                       [sd((T, D), BF)], [pl.BlockSpec((mt, D), row)], [], **cost)
        c0 += w
    return out.reshape(B, S, D), kc.reshape(B, S, kv, hd), vc.reshape(B, S, kv, hd)


def solution(mesh):
    tok = P(("dp", "fsdp"), None, None)
    cache = P(("dp", "fsdp"), None, None, None)
    rowp, gain, table = P("fsdp", None), P("fsdp"), P(None, None)
    return jax.shard_map(functools.partial(local_layer, mesh.shape["fsdp"]), mesh=mesh,
                         in_specs=(tok, gain, rowp, rowp, rowp, rowp, gain, rowp, rowp, rowp, table, table),
                         out_specs=(tok, cache, cache), check_vma=False)
```

time: 747 us -> 661 us (0.88); the launches traced: 736 us -> 660 us
  Pallas kernels: 686 us -> 650 us
  blocking collectives: 24.2 us -> 0 us
  local copies, waits for them, and re-layouts: 20.7 us -> 9.11 us
    pallas_call x16, Pallas kernels: 686 us -> 650 us  [call(): pl.pallas_call(kernel, grid=grid, in_specs=list(in_specs) + [hb] * (len(l...]
    all_gather x1 -> x0, blocking collectives: 24.2 us -> none  [local_layer(): lax.all_gather(jnp.stack([g_attn, g_mlp]), 'fsdp', axis=1, tiled=True)]
where the time goes in v2:
time: 661 us; the launch traced here: 660 us
  Pallas kernels  650 us (98%)
  local copies, waits for them, and re-layouts  9.11 us (1%)
    pallas_call x16, Pallas kernels, call(): pl.pallas_call(kernel, grid=grid, in_specs=list(in_specs) + [hb] * (len(l...  650 us

profile of v2, /device:TPU:112, one launch (start us, length us, event | category | flops | bytes accessed | tf_op | source)
XLA Modules:
  0.0 660.2 jit_solution(2979273445329554587)
XLA Ops:
  0.6 0.7 stack.9
  1.3 0.7 stack.10
  1.9 0.6 fusion.2.refs_1_
  2.6 1.8 copy.59.refs_4_.refs_2_
  4.4 1.8 copy.60.refs_5_.refs_3_
  6.2 48.1 %gather_norm.1 = (bf16[2304,2048]{1,0:T(8,128)(2,1)}, bf16[1,2048]{1,0:T(2,128)(2,1)}, bf16[2048,1024]{1,0:T(8,128)(2,1)}, bf16[2048,256]{1,0:T(8,128)(2,1)}, bf...) custom-call(bf16[2304,2048]{1,0:T(8,128)(2,1)} %bitcast.4, bf16[16,256]{1,0:T(8,128)(2,1)} %fusion.2.refs_1_, ...), custom_call_target="tpu_custom_call" | custom-call | tf_op jit(solution)/shard_map/gather_norm/pallas_call | solution.py:182
  54.4 26.2 %proj0.1 = (bf16[2304,2048]{1,0:T(8,128)(2,1)}, bf16[2304,256]{1,0:T(8,128)(2,1)}, bf16[2304,256]{1,0:T(8,128)(2,1)}, bf16[2048,1024]{1,0:T(8,128)(2,1)}, bf16[2048,2048]{1,0:T(8,128)(2,1)}) custom-call(bf16[2304,2048]{1,0:T(8,128)(2,1)} %get-tuple-element.84.refs_0_, bf16[2048,1024]{1,0:T(8,128)(2,1)} %get-tuple-element.85.refs_1_, ...), custom_call_target="tpu_custom_call", output_to_operand_aliasing={{3}: (7, {})} | custom-call | flops 14495514624 | bytes 18874368 | tf_op jit(solution)/shard_map/proj0/pallas_call | solution.py:182
  80.6 20.1 %proj1.1 = (bf16[2304,2048]{1,0:T(8,128)(2,1)}, bf16[2048,2048]{1,0:T(8,128)(2,1)}) custom-call(bf16[2304,2048]{1,0:T(8,128)(2,1)} %get-tuple-element.84.refs_0_, bf16[2048,1024]{1,0:T(8,128)(2,1)} %get-tuple-element.89.refs_1_, f32[768,64]{1,0:T(8,128)} %copy.59.refs_4_.refs_2_, ...), custom_call_target="tpu_custom_call", output_to_operand_aliasing={{0}: (4, {}), {1}: (5, {})} | custom-call | flops 9663676416 | bytes 18874368 | tf_op jit(solution)/shard_map/proj1/pallas_call | solution.py:182
  100.7 67.7 %attn.1 = (bf16[2304,2048]{1,0:T(8,128)(2,1)}, bf16[2304,2,128]{2,1,0:T(2,128)(2,1)}, bf16[2304,2,128]{2,1,0:T(2,128)(2,1)}, bf16[2048,2048]{1,0:T(8,128)(2,1)},...) custom-call(bf16[2304,2048]{1,0:T(8,128)(2,1)} %get-tuple-element.92, ...), custom_call_target="tpu_custom_call", output_to_operand_aliasing={{3}: (7, {})} | custom-call | flops 28991029248 | bytes 18874368 | tf_op jit(solution)/shard_map/attn/pallas_call | solution.py:182
  168.5 40.2 %wout.1 = (bf16[2304,2048]{1,0:T(8,128)(2,1)}, bf16[2304,2048]{1,0:T(8,128)(2,1)}, bf16[2048,1536]{1,0:T(8,128)(2,1)}, bf16[2048,1536]{1,0:T(8,128)(2,1)}, bf16[...) custom-call(bf16[2304,2048]{1,0:T(8,128)(2,1)} %get-tuple-element.96, ...), custom_call_target="tpu_custom_call", output_to_operand_aliasing={{2}: (6, {}), {3}: (7, {}), {4}: (8, {}), {5}: (9, {})} | custom-call | flops 19327352832 | bytes 37748736 | tf_op jit(solution)/shard_map/wout/pallas_call | solution.py:182
  208.7 40.4 %gateup0.1 = (bf16[2304,11008]{1,0:T(8,128)(2,1)}, bf16[2048,1536]{1,0:T(8,128)(2,1)}, bf16[2048,1536]{1,0:T(8,128)(2,1)}, bf16[2048,1536]{1,0:T(8,128)(2,1)}, b...) custom-call(bf16[2304,2048]{1,0:T(8,128)(2,1)} %get-tuple-element.10, ...), custom_call_target="tpu_custom_call", output_to_operand_aliasing={{1}: (5, {}), {2}: (6, {}), {3}: (7, {}), {4}: (8, {})} | custom-call | flops 28991029248 | bytes 18874368 | tf_op jit(solution)/shard_map/gateup0/pallas_call | solution.py:182
  249.1 40.5 %gateup1.1 = (bf16[2304,11008]{1,0:T(8,128)(2,1)}, bf16[2048,1536]{1,0:T(8,128)(2,1)}, bf16[2048,1536]{1,0:T(8,128)(2,1)}, bf16[2048,1536]{1,0:T(8,128)(2,1)}, b...) custom-call(bf16[2304,2048]{1,0:T(8,128)(2,1)} %get-tuple-element.10, ...), custom_call_target="tpu_custom_call", output_to_operand_aliasing={{0}: (3, {}), {1}: (6, {}), {2}: (7, {}), {3}: (8, {}), {4}... | custom-call | flops 28991029248 | bytes 18874368 | tf_op jit(solution)/shard_map/gateup1/pallas_call | solution.py:182
  289.6 40.5 %gateup2.1 = (bf16[2304,11008]{1,0:T(8,128)(2,1)}, bf16[2048,1536]{1,0:T(8,128)(2,1)}, bf16[2048,1536]{1,0:T(8,128)(2,1)}, bf16[2048,1536]{1,0:T(8,128)(2,1)}, b...) custom-call(bf16[2304,2048]{1,0:T(8,128)(2,1)} %get-tuple-element.10, ...), custom_call_target="tpu_custom_call", output_to_operand_aliasing={{0}: (3, {}), {1}: (6, {}), {2}: (7, {}), {3}: (8, {}), {4}... | custom-call | flops 28991029248 | bytes 18874368 | tf_op jit(solution)/shard_map/gateup2/pallas_call | solution.py:182
  330.1 42.9 %gateup3.1 = (bf16[2304,11008]{1,0:T(8,128)(2,1)}, bf16[2048,1536]{1,0:T(8,128)(2,1)}, bf16[2048,1536]{1,0:T(8,128)(2,1)}, bf16[2048,1536]{1,0:T(8,128)(2,1)}, b...) custom-call(bf16[2304,2048]{1,0:T(8,128)(2,1)} %get-tuple-element.10, ...), custom_call_target="tpu_custom_call", output_to_operand_aliasing={{0}: (3, {}), {1}: (6, {}), {2}: (7, {}), {3}: (8, {}), {4}... | custom-call | flops 28991029248 | bytes 18874368 | tf_op jit(solution)/shard_map/gateup3/pallas_call | solution.py:182
  373.0 44.5 %gateup4.1 = (bf16[2304,11008]{1,0:T(8,128)(2,1)}, bf16[2048,1536]{1,0:T(8,128)(2,1)}, bf16[2048,1536]{1,0:T(8,128)(2,1)}, bf16[2048,1792]{1,0:T(8,128)(2,1)}, b...) custom-call(bf16[2304,2048]{1,0:T(8,128)(2,1)} %get-tuple-element.10, ...), custom_call_target="tpu_custom_call", output_to_operand_aliasing={{0}: (3, {}), {1}: (5, {}), {2}: (6, {}), {3}: (7, {}), {4}... | custom-call | flops 28991029248 | bytes 18874368 | tf_op jit(solution)/shard_map/gateup4/pallas_call | solution.py:182
  417.5 40.2 %gateup5.1 = (bf16[2304,11008]{1,0:T(8,128)(2,1)}, bf16[2048,1792]{1,0:T(8,128)(2,1)}, bf16[2048,1792]{1,0:T(8,128)(2,1)}, bf16[11008,512]{1,0:T(8,128)(2,1)}, bf16[11008,512]{1,0:T(8,128)(2,1)}) custom-call(bf16[2304,2048]{1,0:T(8,128)(2,1)} %get-tuple-element.103.refs_0_, ...), custom_call_target="tpu_custom_call", output_to_operand_aliasing={{0}: (3, {}), {1}: (5, {}), {2}: (6, {}), {3}: (7, {})} | custom-call | flops 28991029248 | bytes 18874368 | tf_op jit(solution)/shard_map/gateup5/pallas_call | solution.py:182
  457.7 45.7 %gateup6.1 = (bf16[2304,11008]{1,0:T(8,128)(2,1)}, bf16[11008,512]{1,0:T(8,128)(2,1)}, bf16[11008,512]{1,0:T(8,128)(2,1)}, bf16[11008,512]{1,0:T(8,128)(2,1)}) custom-call(bf16[2304,2048]{1,0:T(8,128)(2,1)} %get-tuple-element.103.refs_0_, bf16[2048,1792]{1,0:T(8,128)(2,1)} %get-tuple-element.144.refs_1_, ...), custom_call_target="tpu_custom_call", output_to_operand_aliasing={{0}: (3, {}), {1}: (5, {}), {2}: (6, {})} | custom-call | flops 33822867456 | bytes 18874368 | tf_op jit(solution)/shard_map/gateup6/pallas_call | solution.py:182
  503.4 40.6 %down0.1 = (bf16[2304,512]{1,0:T(8,128)(2,1)}, bf16[11008,512]{1,0:T(8,128)(2,1)}, bf16[11008,512]{1,0:T(8,128)(2,1)}, bf16[11008,512]{1,0:T(8,128)(2,1)}) custom-call(bf16[2304,11008]{1,0:T(8,128)(2,1)} %get-tuple-element.149.refs_0_, bf16[11008,512]{1,0:T(8,128)(2,1)} %get-tuple-element.150.refs_1_, ...), custom_call_target="tpu_custom_call", output_to_operand_aliasing={{1}: (4, {}), {2}: (5, {})} | custom-call | flops 25971130368 | bytes 50724864 | tf_op jit(solution)/shard_map/down0/pallas_call | solution.py:182
  544.0 37.2 %down1.1 = (bf16[2304,512]{1,0:T(8,128)(2,1)}, bf16[11008,512]{1,0:T(8,128)(2,1)}, bf16[11008,512]{1,0:T(8,128)(2,1)}) custom-call(bf16[2304,11008]{1,0:T(8,128)(2,1)} %get-tuple-element.149.refs_0_, bf16[11008,512]{1,0:T(8,128)(2,1)} %get-tuple-element.154.refs_1_, ...), custom_call_target="tpu_custom_call", output_to_operand_aliasing={{1}: (3, {}), {2}: (4, {})} | custom-call | flops 25971130368 | bytes 50724864 | tf_op jit(solution)/shard_map/down1/pallas_call | solution.py:182
  581.3 36.9 %down2.1 = (bf16[2304,512]{1,0:T(8,128)(2,1)}, bf16[11008,512]{1,0:T(8,128)(2,1)}) custom-call(bf16[2304,11008]{1,0:T(8,128)(2,1)} %get-tuple-element.149.refs_0_, bf16[11008,512]{1,0:T(8,128)(2,1)} %get-tuple-element.157.refs_1_, bf16[2304,2048]{1,0:T(8,128)(2,1)} %get-tuple-element.151.refs_2_, ...), custom_call_target="tpu_custom_call", output_to_operand_aliasing={{1}: (3, {})} | custom-call | flops 25971130368 | bytes 50724864 | tf_op jit(solution)/shard_map/down2/pallas_call | solution.py:182
  618.2 0.0 copy-start
  618.2 37.8 %down3.1 = bf16[2304,2048]{1,0:T(8,128)(2,1)} custom-call(bf16[2304,11008]{1,0:T(8,128)(2,1)} %get-tuple-element.149.refs_0_, bf16[11008,512]{1,0:T(8,128)(2,1)} %get-tuple-element.159.refs_1_, bf16[2304,2048]{1,0:T(8,128)(2,1)} %get-tuple-element.151.refs_2_, bf16[2304,512]{1,0:T(8,128)(2,1)} %get-tuple-element.160.refs_3_, ...), custom_call_target="tpu_custom_call" | custom-call | flops 25971130368 | bytes 50724864 | tf_op jit(solution)/shard_map/down3/pallas_call | solution.py:182
  656.1 3.1 copy.109
  659.2 0.0 copy-done
  659.2 1.0 copy.110
Async XLA Ops:
  618.2 41.0 %copy-start = (bf16[2304,2,128]{2,1,0:T(2,128)(2,1)S(1)}, bf16[2304,2,128]{2,1,0:T(2,128)(2,1)}, u32[]{:S(2)}) copy-start(bf16[2304,2,128]{2,1,0:T(2,128)(2,1)} %get-tuple-element.164) | copy-start | bytes 3538948
